TPU v7x, 16 devices: a 4x2x1 block of a 4x4x8 slice. The times are simulated.
16 devices in a mesh: rep: 4 (over y, z, core), dp: 4 (over x).
Axes of the slice: x: 4, y: 2, z: 1, core: 2. Of those that a mesh axis runs over, the one named last changes fastest.
The devices are a block of a 4x4x8 slice.
Arguments:
- x: bfloat16 [16, 4096, 1024], P(('rep', 'dp')), parts along dimension 0
- dy: bfloat16 [16, 4096, 1024], P(('rep', 'dp')), parts along dimension 0
- w_gate: bfloat16 [2, 1024, 2816], replicated
- w_up: bfloat16 [2, 1024, 2816], replicated
- w_down: bfloat16 [2, 2816, 1024], replicated
- m_w_gate: float32 [2, 1024, 2816], P(None, 'dp')
- m_w_up: float32 [2, 1024, 2816], P(None, 'dp')
- m_w_down: float32 [2, 2816, 1024], P(None, 'dp')
- v_w_gate: float32 [2, 1024, 2816], P(None, 'dp')
- v_w_up: float32 [2, 1024, 2816], P(None, 'dp')
- v_w_down: float32 [2, 2816, 1024], P(None, 'dp')
Outputs:
- output 1: bfloat16 [8, 1024, 2816], P('rep'), parts along dimension 0
- output 2: bfloat16 [8, 1024, 2816], P('rep'), parts along dimension 0
- output 3: bfloat16 [8, 2816, 1024], P('rep'), parts along dimension 0
- output 4: float32 [8, 1024, 2816], P('rep', 'dp'), parts along dimension 0
- output 5: float32 [8, 1024, 2816], P('rep', 'dp'), parts along dimension 0
- output 6: float32 [8, 2816, 1024], P('rep', 'dp'), parts along dimension 0
- output 7: float32 [8, 1024, 2816], P('rep', 'dp'), parts along dimension 0
- output 8: float32 [8, 1024, 2816], P('rep', 'dp'), parts along dimension 0
- output 9: float32 [8, 2816, 1024], P('rep', 'dp'), parts along dimension 0
There are 4 independent parts. A program takes and returns all parts, laid end to end along the dimension named above; an argument that names none is the same for every part.
All inputs are finite; a program needn't handle non-finite values.
Results may differ from a plain program's by a relative error of at most 0.02.
Values are sent between devices in bfloat16 or wider.
A program may use at most 768 MiB of HBM per device.

v0:
```python
import jax
import jax.numpy as jnp
from jax import lax

NAMES = ("w_gate", "w_up", "w_down")


def matmul(a, w):
    return jnp.dot(a, w, preferred_element_type=jnp.float32).astype(jnp.bfloat16)


def normed(h):
    wide = h.astype(jnp.float32)
    scale = lax.rsqrt(jnp.mean(wide**2, -1, keepdims=True) + 1e-6)
    return (wide * scale).astype(jnp.bfloat16)


def layer(h, w):
    a = normed(h)
    gate = jnp.dot(a, w["w_gate"], preferred_element_type=jnp.float32)
    up = jnp.dot(a, w["w_up"], preferred_element_type=jnp.float32)
    return h + matmul((jax.nn.silu(gate) * up).astype(jnp.bfloat16), w["w_down"])


def adamw(w, m, v, g):
    m = 0.9 * m + 0.1 * g
    v = 0.95 * v + 0.05 * g * g
    step = m * lax.rsqrt(v + 1e-8) + 0.1 * w
    return (w - 0.02 * step).astype(jnp.bfloat16), m, v


def stack(weights, h):
    for number in range(weights["w_gate"].shape[0]):
        h = layer(h, {name: w[number] for name, w in weights.items()})
    return h


def solution(mesh):
    groups = mesh.shape["rep"]

    def step(x, dy, *arrays):
        weights, m, v = (arrays[i : i + 3] for i in (0, 3, 6))
        x, dy = (t.reshape(groups, -1, *t.shape[1:]) for t in (x, dy))

        def of_a_group(x, dy):
            _, back = jax.vjp(lambda w: stack(w, x), dict(zip(NAMES, weights, strict=True)))
            by_weights = back(dy)[0]
            gradients = [by_weights[name].astype(jnp.float32) for name in NAMES]
            new = [adamw(w.astype(jnp.float32), m, v, g) for w, m, v, g in zip(weights, m, v, gradients, strict=True)]
            return tuple(one[which] for which in range(3) for one in new)

        return tuple(t.reshape(-1, *t.shape[2:]) for t in jax.vmap(of_a_group)(x, dy))

    return step
```

profile of v0, /device:TPU:112, one launch (start us, length us, event | category | flops | bytes accessed | tf_op | source)
XLA Modules:
  0.0 1410.0 jit_solution(5899454233344885315)
XLA Ops:
  12.4 11.5 copy
  24.0 32.3 %fusion.104 = f32[4096,2816]{1,0:T(8,128)} fusion(bf16[2,1024,2816]{2,1,0:T(8,128)(2,1)} %param, bf16[1,4096,1024]{2,1,0:T(8,128)(2,1)} %param.2, f32[4096]{0:T(1024)S(1)} %add_rsqrt_fusion), kind=kOutput, calls=%fused_computation.120 | convolution fusion | flops 23634903040 | bytes 60309504 | tf_op jit(solution)/vmap(jvp())/dot_general | solution.py:20
  56.3 30.5 %fusion.102 = f32[4096,2816]{1,0:T(8,128)} fusion(bf16[2,1024,2816]{2,1,0:T(8,128)(2,1)S(1)} %bitcast.389, bf16[1,4096,1024]{2,1,0:T(8,128)(2,1)} %param.2, f32[4096]{0:T(1024)S(1)} %add_rsqrt_fusion), kind=kOutput, calls=%fused_computation.118 | convolution fusion | flops 23634903040 | bytes 60309504 | tf_op jit(solution)/vmap(jvp())/dot_general | solution.py:21
  86.9 38.0 %fusion.26 = bf16[4096,2816]{1,0:T(8,128)(2,1)} fusion(f32[4096,2816]{1,0:T(8,128)} %fusion.102, f32[4096,2816]{1,0:T(8,128)} %fusion.104), kind=kLoop, calls=%fused_computation.39 | loop fusion | flops 69206016 | bytes 115343360
  124.9 32.6 %fusion.39 = (f32[4096]{0:T(1024)S(1)}, bf16[1,1,4096,1024]{2,3,1,0:T(8,128)(2,1)}) fusion(bf16[4096,2816]{1,0:T(8,128)(2,1)} %fusion.26, bf16[2,2816,1024]{2,1,0:T(8,128)(2,1)} %param.4, bf16[1,4096,1024]{1,2,0:T(8,128)(2,1)} %copy), kind=kOutput, calls=%fused_computation.56 | convolution fusion | flops 23643287552 | bytes 45629440 | tf_op jit(solution)/vmap(jvp())/dot_general | solution.py:9
  158.1 33.0 %fusion.92 = f32[4096,2816]{1,0:T(8,128)} fusion(bf16[1,1,4096,1024]{2,3,1,0:T(8,128)(2,1)} %get-tuple-element.10, f32[4096]{0:T(1024)S(1)} %bitcast.393, bf16[2,1024,2816]{2,1,0:T(8,128)(2,1)} %param), kind=kOutput, calls=%fused_computation.108 | convolution fusion | flops 23634903040 | bytes 60309504 | tf_op jit(solution)/vmap(jvp())/dot_general | solution.py:20
  191.1 31.8 %fusion.96 = f32[4096,2816]{1,0:T(8,128)} fusion(bf16[1,1,4096,1024]{2,3,1,0:T(8,128)(2,1)S(1)} %copy-done.1, f32[4096]{0:T(1024)S(1)} %bitcast.394, bf16[2,1024,2816]{2,1,0:T(8,128)(2,1)} %param.3), kind=kOutput, calls=%fused_computation.112 | convolution fusion | flops 23634903040 | bytes 60309504 | tf_op jit(solution)/vmap(jvp())/dot_general | solution.py:21
  222.9 31.4 %convolution_convert_fusion.1 = bf16[4096,2816]{1,0:T(8,128)(2,1)} fusion(bf16[1,4096,1024]{2,1,0:T(8,128)(2,1)} %param.5, bf16[2,2816,1024]{2,1,0:T(8,128)(2,1)} %param.4), kind=kOutput, calls=%fused_computation.48 | convolution fusion | flops 23633854464 | bytes 37224448 | tf_op jit(solution)/vmap(transpose(jvp()))/dot_general | solution.py:9
  254.3 11.9 copy.1
  266.2 45.2 %fusion.6 = bf16[4096,2816]{1,0:T(8,128)(2,1)} fusion(f32[4096,2816]{1,0:T(8,128)} %fusion.92, f32[4096,2816]{1,0:T(8,128)} %fusion.96, bf16[4096,2816]{1,0:T(8,128)(2,1)} %convolution_convert_fusion.1), kind=kLoop, calls=%fused_computation.11 | loop fusion | flops 138412032 | bytes 138412032
  311.4 30.4 %fusion.94 = bf16[4096,1024]{0,1:T(8,128)(2,1)} fusion(bf16[4096,2816]{1,0:T(8,128)(2,1)} %fusion.6, bf16[2,1024,2816]{2,1,0:T(8,128)(2,1)} %param), kind=kOutput, calls=%fused_computation.110 | convolution fusion | flops 23622320128 | bytes 37224448 | tf_op jit(solution)/vmap(transpose(jvp()))/dot_general | solution.py:20
  341.8 39.3 %fusion.41 = (f32[4096]{0:T(1024)S(1)}, bf16[4096,1024]{0,1:T(8,128)(2,1)}) fusion(bf16[1,1,4096,1024]{2,3,1,0:T(8,128)(2,1)} %get-tuple-element.10, bf16[4096,1024]{0,1:T(8,128)(2,1)} %fusion.94, bf16[2,1024,2816]{2,1,0:T(8,128)(2,1)} %param.3, bf16[4096,2816]{1,0:T(8,128)(2,1)} %convolution_convert_fusion.1, f32[4096,2816]{1,0:T(8,128)} %fusion.92), kind=kOutput, calls=%fused_computation.58 | convolution fusion | flops 23716687872 | bytes 100155392 | tf_op jit(solution)/vmap(transpose(jvp()))/dot_general | solution.py:21
  381.2 12.0 fusion.45
  393.2 33.7 %convolution_bitcast_fusion.1 = f32[1,2816,1024]{2,1,0:T(8,128)} fusion(bf16[4096,2816]{1,0:T(8,128)(2,1)} %fusion.26, bf16[4096,1024]{0,1:T(8,128)(2,1)} %fusion.45), kind=kOutput, calls=%fused_computation.86 | convolution fusion | flops 23622320128 | bytes 42991616 | tf_op jit(solution)/vmap(transpose(jvp()))/dot_general | solution.py:9
  427.0 45.7 %fusion.53 = f32[1,2816,1024]{2,1,0:T(8,128)} fusion(bf16[1,4096,1024]{2,1,0:T(8,128)(2,1)} %param.5, f32[4096,2816]{1,0:T(8,128)} %fusion.96, f32[4096,2816]{1,0:T(8,128)} %fusion.92), kind=kOutput, calls=%fused_computation.81 | convolution fusion | flops 23691526144 | bytes 112197632 | tf_op jit(solution)/vmap(transpose(jvp()))/dot_general | solution.py:9
  472.9 30.8 %convolution_convert_fusion = bf16[4096,2816]{1,0:T(8,128)(2,1)} fusion(bf16[4096,1024]{0,1:T(8,128)(2,1)} %fusion.45, bf16[2,2816,1024]{2,1,0:T(8,128)(2,1)} %param.4), kind=kOutput, calls=%fused_computation.47 | convolution fusion | flops 23633854464 | bytes 37224448 | tf_op jit(solution)/vmap(transpose(jvp()))/dot_general | solution.py:9
  503.8 37.6 %fusion.66 = f32[1,1024,2816]{2,1,0:T(8,128)} fusion(bf16[4096,2816]{1,0:T(8,128)(2,1)} %convolution_convert_fusion, f32[4096,2816]{1,0:T(8,128)} %fusion.104, bf16[1,4096,1024]{1,2,0:T(8,128)(2,1)} %copy, f32[4096]{0:T(1024)S(1)} %copy-done.8), kind=kOutput, calls=%fused_computation.85 | convolution fusion | flops 23704109056 | bytes 89145344 | tf_op jit(solution)/vmap(transpose(jvp()))/dot_general | solution.py:21
  542.0 37.6 %fusion.58 = f32[1,1024,2816]{2,1,0:T(8,128)} fusion(bf16[4096,2816]{1,0:T(8,128)(2,1)} %convolution_convert_fusion.1, f32[4096,2816]{1,0:T(8,128)} %fusion.92, bf16[1,1,4096,1024]{2,3,1,0:T(8,128)(2,1)} %get-tuple-element.10, f32[4096]{0:T(1024)S(1)} %bitcast.396), kind=kOutput, calls=%fused_computation.82 | convolution fusion | flops 23704109056 | bytes 89145344 | tf_op jit(solution)/vmap(transpose(jvp()))/dot_general | solution.py:21
  579.8 33.2 %convolution_bitcast_fusion = f32[1,1024,2816]{2,1,0:T(8,128)} fusion(bf16[4096,2816]{1,0:T(8,128)(2,1)} %fusion.6, bf16[1,1,4096,1024]{2,3,1,0:T(8,128)(2,1)} %get-tuple-element.10, f32[4096]{0:T(1024)S(1)} %bitcast.397), kind=kOutput, calls=%fused_computation.84 | convolution fusion | flops 23634903040 | bytes 43008000 | tf_op jit(solution)/vmap(transpose(jvp()))/dot_general | solution.py:20
  613.1 45.8 %fusion.61 = f32[1,1024,2816]{2,1,0:T(8,128)} fusion(f32[4096,2816]{1,0:T(8,128)} %fusion.104, f32[4096,2816]{1,0:T(8,128)} %fusion.102, bf16[4096,2816]{1,0:T(8,128)(2,1)} %convolution_convert_fusion, bf16[1,4096,1024]{1,2,0:T(8,128)(2,1)} %copy, f32[4096]{0:T(1024)S(1)} %copy-done.8), kind=kOutput, calls=%fused_computation.83 | convolution fusion | flops 23761780736 | bytes 135282688 | tf_op jit(solution)/vmap(transpose(jvp()))/dot_general | solution.py:20
  665.0 10.0 fusion.124
  675.1 65.5 %reduce-scatter.25.cloned.1.call-done = f32[1,256,2816]{2,1,0:T(8,128)} async-done(((f32[1,1024,2816]{2,1,0:T(8,128)}), f32[1,256,2816]{2,1,0:T(8,128)}) %reduce-scatter.25.cloned.1.call-update) | async-done | bytes 2883600
  742.5 101.9 %reduce-scatter.23.cloned.1.call-done = f32[1,256,2816]{2,1,0:T(8,128)} async-done(((f32[1,1024,2816]{2,1,0:T(8,128)}), f32[1,256,2816]{2,1,0:T(8,128)}) %reduce-scatter.23.cloned.1.call-update) | async-done | bytes 2883600
  846.4 9.8 fusion.125
  856.4 92.5 %reduce-scatter.19.cloned.1.call-done = f32[1,256,2816]{2,1,0:T(8,128)} async-done(((f32[1,1024,2816]{2,1,0:T(8,128)}), f32[1,256,2816]{2,1,0:T(8,128)}) %reduce-scatter.19.cloned.1.call-update) | async-done | bytes 2883600
  950.9 102.5 %reduce-scatter.21.cloned.1.call-done = f32[1,256,2816]{2,1,0:T(8,128)} async-done(((f32[1,1024,2816]{2,1,0:T(8,128)}), f32[1,256,2816]{2,1,0:T(8,128)}) %reduce-scatter.21.cloned.1.call-update) | async-done | bytes 2883600
  1055.4 9.8 fusion.126
  1065.2 95.5 %all-gather.14.cloned.1.call-done = bf16[1,2,2816,1024]{3,2,1,0:T(8,128)(2,1)} async-done(((bf16[1,2,704,1024]{3,2,1,0:T(8,128)(2,1)}), bf16[1,2,2816,1024]{3,2,1,0:T(8,128)(2,1)}) %all-gather.14.cloned.1.call-update) | async-done | bytes 11534352 | tf_op jit(solution)/reshape | solution.py:52
  1160.7 109.2 %all-gather.12.cloned.1.call-done = bf16[1,2,1024,2816]{3,2,1,0:T(8,128)(2,1)} async-done(((bf16[1,2,256,2816]{3,2,1,0:T(8,128)(2,1)}), bf16[1,2,1024,2816]{3,2,1,0:T(8,128)(2,1)}) %all-gather.12.cloned.1.call-update) | async-done | bytes 11534352 | tf_op jit(solution)/reshape | solution.py:52
  1269.9 109.2 %all-gather.10.cloned.1.call-done = bf16[1,2,1024,2816]{3,2,1,0:T(8,128)(2,1)} async-done(((bf16[1,2,256,2816]{3,2,1,0:T(8,128)(2,1)}), bf16[1,2,1024,2816]{3,2,1,0:T(8,128)(2,1)}) %all-gather.10.cloned.1.call-update) | async-done | bytes 11534352 | tf_op jit(solution)/reshape | solution.py:52
  1379.1 11.7 copy.5
  1390.7 5.8 copy.6
  (72 shorter events, 26.9 us)
Async XLA Ops:
  7.2 653.7 %reduce-scatter.29.cloned.1.call-start = ((), (), s32[]{:S(2)}) async-start(), calls=%async_computation.14 | async-start | bytes 14417920
  12.3 43.9 %slice-start.5 = ((s8[11534336]{0:T(1024)(128)(4,1)}), s8[3145728]{0:T(1024)(128)(4,1)S(1)}, s32[]{:S(2)}) async-start(s8[11534336]{0:T(1024)(128)(4,1)} %bitcast.388), calls=%async_computation.20 | async-start | bytes 6291456
  23.9 32.4 %copy-start.7 = (f32[4096]{0:T(1024)}, f32[4096]{0:T(1024)S(1)}, u32[]{:S(2)}) copy-start(f32[4096]{0:T(1024)S(1)} %add_rsqrt_fusion) | copy-start | bytes 49156
  23.9 32.4 %slice-start.6 = ((s8[11534336]{0:T(1024)(128)(4,1)}), s8[4194304]{0:T(1024)(128)(4,1)S(1)}, s32[]{:S(2)}) async-start(s8[11534336]{0:T(1024)(128)(4,1)} %bitcast.388), calls=%async_computation.21 | async-start | bytes 8388608
  23.9 32.4 %slice-start.7 = ((s8[11534336]{0:T(1024)(128)(4,1)}), s8[4194304]{0:T(1024)(128)(4,1)S(1)}, s32[]{:S(2)}) async-start(s8[11534336]{0:T(1024)(128)(4,1)} %bitcast.388), calls=%async_computation.22 | async-start | bytes 8388608
  157.5 0.6 copy-start.2
  157.5 33.5 %copy-start.4 = (f32[1,1,4096]{2,1,0:T(1,128)}, f32[1,1,4096]{2,1,0:T(1,128)S(1)}, u32[]{:S(2)}) copy-start(f32[1,1,4096]{2,1,0:T(1,128)S(1)} %rsqrt.31) | copy-start | bytes 49156
  158.1 33.0 %copy-start.1 = (bf16[1,1,4096,1024]{2,3,1,0:T(8,128)(2,1)S(1)}, bf16[1,1,4096,1024]{2,3,1,0:T(8,128)(2,1)}, u32[]{:S(2)}) copy-start(bf16[1,1,4096,1024]{2,3,1,0:T(8,128)(2,1)} %get-tuple-element.10) | copy-start | bytes 25165828
  311.4 69.7 %slice-start = ((s8[8388608]{0:T(1024)(128)(4,1)}), s8[4194304]{0:T(1024)(128)(4,1)S(1)}, s32[]{:S(2)}) async-start(s8[8388608]{0:T(1024)(128)(4,1)} %bitcast.381), calls=%async_computation.15 | async-start | bytes 8388608
  341.8 39.3 %copy-start.3 = (f32[4096]{0:T(1024)S(1)}, f32[4096]{0:T(1024)}, u32[]{:S(2)}) copy-start(f32[4096]{0:T(1024)} %copy-done.2) | copy-start | bytes 49156
  341.8 39.4 %slice-start.1 = ((s8[8388608]{0:T(1024)(128)(4,1)}), s8[4194304]{0:T(1024)(128)(4,1)S(1)}, s32[]{:S(2)}) async-start(s8[8388608]{0:T(1024)(128)(4,1)} %bitcast.381), calls=%async_computation.16 | async-start | bytes 8388608
  341.8 39.4 %copy-start.5 = (f32[1,1,4096]{2,1,0:T(1,128)S(1)}, f32[1,1,4096]{2,1,0:T(1,128)}, u32[]{:S(2)}) copy-start(f32[1,1,4096]{2,1,0:T(1,128)} %copy-done.4) | copy-start | bytes 49156
  427.0 236.0 %reduce-scatter.27.cloned.1.call-start = ((), (), s32[]{:S(2)}) async-start(), calls=%async_computation.13 | async-start | bytes 14417920
  472.8 30.9 %copy-start.8 = (f32[4096]{0:T(1024)S(1)}, f32[4096]{0:T(1024)}, u32[]{:S(2)}) copy-start(f32[4096]{0:T(1024)} %copy-done.7) | copy-start | bytes 49156
  472.8 267.7 %reduce-scatter.25.cloned.1.call-start = ((), (), s32[]{:S(2)}) async-start(), calls=%async_computation.12 | async-start | bytes 14417920
  541.3 0.7 copy-start.6
  541.4 303.1 %reduce-scatter.23.cloned.1.call-start = ((), (), s32[]{:S(2)}) async-start(), calls=%async_computation.11 | async-start | bytes 14417920
  579.7 369.2 %reduce-scatter.19.cloned.1.call-start = ((), (), s32[]{:S(2)}) async-start(), calls=%async_computation.9 | async-start | bytes 14417920
  613.1 440.3 %reduce-scatter.21.cloned.1.call-start = ((), (), s32[]{:S(2)}) async-start(), calls=%async_computation.10 | async-start | bytes 14417920
  659.0 0.7 copy-start.9
  659.0 501.7 %all-gather.14.cloned.1.call-start = ((), (), s32[]{:S(2)}) async-start(), calls=%async_computation.8 | async-start | bytes 14417920 | tf_op jit(solution)/reshape | solution.py:52
  675.0 594.9 %all-gather.12.cloned.1.call-start = ((), (), s32[]{:S(2)}) async-start(), calls=%async_computation.7 | async-start | bytes 14417920 | tf_op jit(solution)/reshape | solution.py:52
  856.3 522.8 %all-gather.10.cloned.1.call-start = ((), (), s32[]{:S(2)}) async-start(), calls=%async_computation.6 | async-start | bytes 14417920 | tf_op jit(solution)/reshape | solution.py:52
  1379.1 11.7 copy-start
  1379.1 17.5 %slice-start.2 = ((s8[11534336]{0:T(1024)(128)(4,1)}), s8[4194304]{0:T(1024)(128)(4,1)S(1)}, s32[]{:S(2)}) async-start(s8[11534336]{0:T(1024)(128)(4,1)} %bitcast.383), calls=%async_computation.17 | async-start | bytes 8388608
  1379.1 18.3 %slice-start.3 = ((s8[11534336]{0:T(1024)(128)(4,1)}), s8[4194304]{0:T(1024)(128)(4,1)S(1)}, s32[]{:S(2)}) async-start(s8[11534336]{0:T(1024)(128)(4,1)} %bitcast.383), calls=%async_computation.18 | async-start | bytes 8388608
  1390.7 7.9 slice-start.4
Sparse Core Ops, SparseCore 0:
  427.1 104.8 reduce-scatter.28
  534.3 101.6 reduce-scatter.26
  638.9 101.6 reduce-scatter.24
  742.8 101.6 reduce-scatter.22
  847.2 101.6 reduce-scatter.18
  951.7 101.6 reduce-scatter.20
  1054.9 105.7 all-gather.13
  1162.9 106.9 all-gather.11
  1272.0 106.9 all-gather.9
where the time goes:
time: 1420 us; the launch traced here: 1410 us
  waiting for transfers between devices  677 us (48%)
  matrix products  526 us (37%)
  other arithmetic  142 us (10%)
  local copies, waits for them, and re-layouts  49.7 us (4%)
  between operations  15.2 us (1%)
    unnamed x15, waiting for transfers between devices  363 us
    reshape x3, waiting for transfers between devices, step(): t.reshape(-1, *t.shape[2:])  314 us
    dot_general x5, matrix products, layer(): up = jnp.dot(a, w['w_up'], preferred_element_type=jnp.float32)  177 us
    dot_general x5, matrix products, layer(): gate = jnp.dot(a, w['w_gate'], preferred_element_type=jnp.float32)  175 us
    dot_general x5, matrix products, matmul(): jnp.dot(a, w, preferred_element_type=jnp.float32).astype(jnp.bfloat16)  174 us
    unnamed x6, other arithmetic  95.2 us
    unnamed x41, local copies, waits for them, and re-layouts  49.1 us
    reshape x3, other arithmetic, step(): t.reshape(-1, *t.shape[2:])  29.6 us
  transfers between devices with their start and end apart: 9, of which 7 were waited for; matrix products, arithmetic and copies ran while one was open for 19% of the time, Pallas kernels for 0%

commit v1 on v0

v1 whole, which is shorter than its diff:
```python
import functools

import jax
import jax.numpy as jnp
from jax import lax
from jax.experimental import pallas as pl
from jax.experimental.pallas import tpu as pltpu
from jax.sharding import PartitionSpec as P

F32, BF16 = jnp.float32, jnp.bfloat16
BLOCK = 256
UNIT = 64
MIB = 2**20
TM = 512
ANY = pl.BlockSpec(memory_space=pl.ANY)


def dot(a, b):
    return jnp.dot(a, b, preferred_element_type=F32)


def norm_scale(wide):
    return lax.rsqrt(jnp.mean(wide * wide, -1, keepdims=True) + 1e-6)


def params(limit=60):
    return pltpu.CompilerParams(vmem_limit_bytes=limit * MIB, dimension_semantics=("arbitrary",))


def forward_kernel(blocks, x_ref, wg_hbm, wu_hbm, wd_hbm, a0_ref, h_ref, a1_ref, wg, wu, wd, act, sems):
    step = pl.program_id(0)

    def copies(b):
        cols = pl.ds(b * BLOCK, BLOCK)
        return (
            pltpu.make_async_copy(wg_hbm.at[0, :, cols], wg.at[:, cols], sems.at[0, b]),
            pltpu.make_async_copy(wu_hbm.at[0, :, cols], wu.at[:, cols], sems.at[1, b]),
            pltpu.make_async_copy(wd_hbm.at[0, cols, :], wd.at[cols, :], sems.at[2, b]),
        )

    @pl.when(step == 0)
    def _():
        for b in range(blocks):
            for c in copies(b):
                c.start()

    wide = x_ref[...].astype(F32)
    a0_ref[...] = (wide * norm_scale(wide)).astype(BF16)

    @pl.when(step == 0)
    def _():
        for b in range(blocks):
            for c in copies(b):
                c.wait()

    for b in range(blocks):
        cols = slice(b * BLOCK, (b + 1) * BLOCK)
        gate = dot(a0_ref[...], wg[:, cols])
        up = dot(a0_ref[...], wu[:, cols])
        act[:, cols] = (gate * jax.nn.sigmoid(gate) * up).astype(BF16)
    h = x_ref[...] + dot(act[...], wd[...]).astype(BF16)
    h_ref[...] = h
    wide = h.astype(F32)
    a1_ref[...] = (wide * norm_scale(wide)).astype(BF16)


def forward(x, wg, wu, wd, tm=None):
    tm = tm or TM
    t, d = x.shape
    ff = wg.shape[-1]
    blocks = ff // BLOCK
    tile = pl.BlockSpec((tm, d), lambda i: (i, 0))
    return pl.pallas_call(
        functools.partial(forward_kernel, blocks),
        grid=(t // tm,),
        in_specs=[tile, ANY, ANY, ANY],
        out_specs=[tile] * 3,
        out_shape=[jax.ShapeDtypeStruct((t, d), BF16)] * 3,
        scratch_shapes=[
            pltpu.VMEM((d, ff), BF16),
            pltpu.VMEM((d, ff), BF16),
            pltpu.VMEM((ff, d), BF16),
            pltpu.VMEM((tm, ff), BF16),
            pltpu.SemaphoreType.DMA((3, blocks)),
        ],
        compiler_params=params(),
        cost_estimate=pl.CostEstimate(flops=6 * t * d * ff, bytes_accessed=8 * t * d + 6 * d * ff, transcendentals=t * ff),
        name="forward",
    )(x, wg, wu, wd)


def adamw(w, m, v, g):
    m = 0.9 * m + 0.1 * g
    v = 0.95 * v + 0.05 * g * g
    step = m * lax.rsqrt(v + 1e-8) + 0.1 * w
    return (w - 0.02 * step).astype(BF16), m, v


GU, DOWN, LAST = 0, 1, 2
RING = 4
PACKS = 17


def pack_kind(p):
    r = lax.rem(p, PACKS)
    down = ((r >= 4) & (r < 6)) | ((r >= 10) & (r < 12))
    last = r >= 15
    return {GU: jnp.logical_not(down | last), DOWN: down, LAST: last}


def backward_kernel(
    n, steps, d, ff, axis,
    a1_hbm, dy_hbm, h1_hbm, a0_hbm, wg_hbm, wu_hbm, wd_hbm, mg_hbm, mu_hbm, md_hbm, vg_hbm, vu_hbm, vd_hbm,
    ng_hbm, nu_hbm, nd_hbm, mg_out, mu_out, md_out, vg_out, vu_out, vd_out, dh_hbm,
    tiles, at, dht, wgu, wdn, wdt, wgut, accgu, accd, da, dbuf, hout,
    send, keep, own, r1, r2, s2, wnew, mvin, win, mvout,
    tile_sem, weight_sem, hout_sem, s1s, s1r, s2s, s2r, g1s, g1r, g2s, g2r, loc_sem, mvin_sem, mvout_sem,
):
    tm = tiles.shape[2]
    blocks = ff // BLOCK
    q = BLOCK
    me = lax.axis_index(axis)
    right, left, far = (lax.rem(me + k, n) for k in (1, n - 1, 2))
    to = ({axis: right}, {axis: left})
    mult = pl.multiple_of

    barrier = pltpu.get_barrier_semaphore()
    for dev in to:
        pl.semaphore_signal(barrier, inc=1, device_id=dev, device_id_type=pl.DeviceIdType.MESH)
    pl.semaphore_wait(barrier, 2)


    def layer_of(p):
        return 1 - p // PACKS

    def gu_cols(p):
        r = lax.rem(p, PACKS)
        i = jnp.where(r < 4, r, jnp.where(r < 10, r - 2, r - 4))
        return mult((3 * lax.rem(i, 4) + i // 4) * q, q)

    def down_cols(kind, p, half):
        r = lax.rem(p, PACKS)
        first = r - 15 if kind == LAST else jnp.where(r < 6, r - 4, r - 10)
        return mult((2 * first + half) * q, q)

    def down_row(p, dev):
        r = lax.rem(p, PACKS)
        return mult(jnp.where(r < 6, 0, 4 * UNIT) + dev * UNIT, UNIT)

    def last_row(dev, u):
        return mult(jnp.where(u < dev, u, 8 + u) * UNIT, UNIT)

    def height(kind):
        return 3 * UNIT if kind == LAST else q

    def rows_in(kind, p, dev, half, ref_gu, ref_d, per_device):
        lay = layer_of(p)
        if kind == GU:
            base = 0 if per_device else mult(dev * q, q)
            return [(ref_gu[half].at[lay, pl.ds(base, q), pl.ds(gu_cols(p), q)], 0, q)]
        cols = pl.ds(down_cols(kind, p, half), q)
        base = 0 if per_device else dev * (ff // n)
        if kind == DOWN:
            return [(ref_d.at[lay, pl.ds(mult(base + down_row(p, dev), UNIT), q), cols], 0, q)]
        return [(ref_d.at[lay, pl.ds(mult(base + last_row(dev, u), UNIT), UNIT), cols], u * UNIT, UNIT) for u in range(3)]

    def new_pieces(kind, p, dev, half):
        return rows_in(kind, p, dev, half, (ng_hbm, nu_hbm), nd_hbm, False)


    def s1_copy(kind, p, way):
        s, h = lax.rem(p, RING), height(kind)
        rows = pl.ds(0, 2 * h)
        return pltpu.make_async_remote_copy(
            send.at[s, way, rows], r1.at[s, way, rows], s1s.at[way, s], s1r.at[way, s], to[way], pl.DeviceIdType.MESH
        )

    def s2_copy(kind, p, way):
        s, h = lax.rem(p, RING), height(kind)
        rows = pl.ds(0, h)
        return pltpu.make_async_remote_copy(
            s2.at[s, way, rows], r2.at[s, way, rows], s2s.at[way, s], s2r.at[way, s], to[way], pl.DeviceIdType.MESH
        )

    def g1_copies(kind, p, way, half):
        s = lax.rem(p, RING)
        return [
            pltpu.make_async_remote_copy(
                wnew.at[s, half, pl.ds(at_, size)], view, g1s.at[way, half, s], g1r.at[way, half, s], to[way], pl.DeviceIdType.MESH
            )
            for view, at_, size in new_pieces(kind, p, me, half)
        ]

    def g2_copies(kind, p, way):
        s, dev = lax.rem(p, 2 * RING), (left, right)[way]
        return [
            pltpu.make_async_remote_copy(view, view, g2s.at[way, s], g2r.at[way, s], to[way], pl.DeviceIdType.MESH)
            for view, _, _ in new_pieces(kind, p, dev, way)
        ]

    def total_of(kind, p, way, half, sems, side):
        s, h = lax.rem(p, RING), height(kind)
        ref = wnew.at[s, half, pl.ds(0, h)]
        copy = pltpu.make_async_remote_copy(ref, ref, sems[0], sems[1], to[way], pl.DeviceIdType.MESH)
        copy.wait_send() if side == 0 else copy.wait_recv()

    def moment_loads(kind, p):
        b, s = lax.rem(p, 2), []
        for half in range(2):
            for k, (gu, dn) in enumerate((((mg_hbm, mu_hbm), md_hbm), ((vg_hbm, vu_hbm), vd_hbm))):
                for view, at_, size in rows_in(kind, p, me, half, gu, dn, True):
                    s.append(pltpu.make_async_copy(view, mvin.at[b, 2 * half + k, pl.ds(at_, size)], mvin_sem.at[b, 2 * half + k]))
            for view, at_, size in rows_in(kind, p, me, half, (wg_hbm, wu_hbm), wd_hbm, False):
                s.append(pltpu.make_async_copy(view, win.at[b, half, pl.ds(at_, size)], mvin_sem.at[b, 4 + half]))
        return s

    def moment_loads_wait(kind, p):
        b, rows = lax.rem(p, 2), pl.ds(0, height(kind))
        for k in range(4):
            pltpu.make_async_copy(mvin.at[b, k, rows], mvin.at[b, k, rows], mvin_sem.at[b, k]).wait()
        for half in range(2):
            pltpu.make_async_copy(win.at[b, half, rows], win.at[b, half, rows], mvin_sem.at[b, 4 + half]).wait()

    def moment_stores(kind, p):
        b, s = lax.rem(p, 2), []
        for half in range(2):
            for k, (gu, dn) in enumerate((((mg_out, mu_out), md_out), ((vg_out, vu_out), vd_out))):
                for view, at_, size in rows_in(kind, p, me, half, gu, dn, True):
                    s.append(pltpu.make_async_copy(mvout.at[b, 2 * half + k, pl.ds(at_, size)], view, mvout_sem.at[b, 2 * half + k]))
        return s

    def moment_stores_wait(kind, p):
        b, rows = lax.rem(p, 2), pl.ds(0, height(kind))
        for k in range(4):
            pltpu.make_async_copy(mvout.at[b, k, rows], mvout.at[b, k, rows], mvout_sem.at[b, k]).wait()

    def own_copies(kind, p):
        s = lax.rem(p, RING)
        return [
            pltpu.make_async_copy(wnew.at[s, half, pl.ds(at_, size)], view, loc_sem.at[half, s])
            for half in range(2)
            for view, at_, size in new_pieces(kind, p, me, half)
        ]

    def stage(kind, p):
        s, h = lax.rem(p, RING), height(kind)
        if kind == GU:
            def part(dev, half):
                return accgu[pl.ds(mult(dev * q, q), q), half * q : (half + 1) * q].astype(BF16)
        else:
            def part(dev, half):
                return dbuf[pl.ds(mult(dev * h, UNIT), h), pl.ds(down_cols(kind, p, half), q)]
        send[s, 0, :h, :] = part(far, 0)
        send[s, 0, h : 2 * h, :] = part(right, 1)
        send[s, 1, :h, :] = part(far, 1)
        send[s, 1, h : 2 * h, :] = part(left, 0)
        keep[s, 0, :h, :] = part(right, 0)
        keep[s, 1, :h, :] = part(left, 1)
        own[s, 0, :h, :] = part(me, 0)
        own[s, 1, :h, :] = part(me, 1)

    def do_s1(kind, p):
        stage(kind, p)
        for c in moment_loads(kind, p):
            c.start()
        for way in range(2):
            s1_copy(kind, p, way).start()

    def do_s2(kind, p):
        s, h = lax.rem(p, RING), height(kind)
        for way in range(2):
            s1_copy(kind, p, way).wait_recv()
            s2[s, way, :h, :] = (keep[s, way, :h, :].astype(F32) + r1[s, way, :h, :].astype(F32)).astype(BF16)
            s2_copy(kind, p, way).start()

    def do_s3(kind, p):
        s, b, h = lax.rem(p, RING), lax.rem(p, 2), height(kind)
        moment_loads_wait(kind, p)
        for k, cond in pack_kind(p - 2).items():
            @pl.when(cond & (p >= 2))
            def _():
                moment_stores_wait(k, p - 2)
        for way in range(2):
            s2_copy(kind, p, way).wait_recv()

        def rows_of(u, _):
            rows = pl.ds(mult(u * UNIT, UNIT), UNIT)
            rest = pl.ds(mult(h + u * UNIT, UNIT), UNIT)
            for half in range(2):
                g = own[s, half, rows, :].astype(F32) + r1[s, 1 - half, rest, :].astype(F32) + r2[s, half, rows, :].astype(F32)
                g = g.astype(BF16).astype(F32)
                w, m, v = adamw(win[b, half, rows, :].astype(F32), mvin[b, 2 * half, rows, :], mvin[b, 2 * half + 1, rows, :], g)
                wnew[s, half, rows, :] = w
                mvout[b, 2 * half, rows, :] = m
                mvout[b, 2 * half + 1, rows, :] = v
            return 0

        lax.fori_loop(0, h // UNIT, rows_of, 0)
        for c in moment_stores(kind, p):
            c.start()
        for way in range(2):
            for half in ((0, 1), (1, 0))[way]:
                for c in g1_copies(kind, p, way, half):
                    c.start()
        for c in own_copies(kind, p):
            c.start()

    def do_s4(kind, p):
        s = lax.rem(p, RING)
        for way in range(2):
            s1_copy(kind, p, way).wait_send()
            s2_copy(kind, p, way).wait_send()
            for half in ((0, 1), (1, 0))[way]:
                total_of(kind, p, way, half, (g1s.at[way, half, s], g1r.at[way, half, s]), 1)
                if half == way:
                    for c in g2_copies(kind, p, way):
                        c.start()

    def do_s5(kind, p):
        s, rows = lax.rem(p, RING), pl.ds(0, height(kind))
        for way in range(2):
            for half in range(2):
                total_of(kind, p, way, half, (g1s.at[way, half, s], g1r.at[way, half, s]), 0)
            far_s = lax.rem(p, 2 * RING)
            total_of(kind, p, way, way, (g2s.at[way, far_s], g2r.at[way, far_s]), 1)
            total_of(kind, p, way, way, (g2s.at[way, far_s], g2r.at[way, far_s]), 0)
        for half in range(2):
            pltpu.make_async_copy(wnew.at[s, half, rows], wnew.at[s, half, rows], loc_sem.at[half, s]).wait()

    def each(do, p, among=(GU, DOWN, LAST)):
        for kind, cond in pack_kind(p).items():
            if kind in among:
                @pl.when(cond & (p >= 0) & (p < 2 * PACKS))
                def _():
                    do(kind, p)

    def full(p, among=(GU, DOWN, LAST)):
        each(do_s1, p, among)
        each(do_s3, p - 1)

    def half(p):
        each(do_s2, p)
        each(do_s4, p - 2)
        each(do_s5, p - 4)


    def weight_loads(it):
        b, lay = lax.rem(it, 2), 1 - it // blocks
        i = lax.rem(it, blocks)
        cols = pl.ds(mult((3 * lax.rem(i, 4) + i // 4) * q, q), q)
        return (
            pltpu.make_async_copy(wg_hbm.at[lay, :, cols], wgu.at[b, :, pl.ds(0, q)], weight_sem.at[b, 0]),
            pltpu.make_async_copy(wu_hbm.at[lay, :, cols], wgu.at[b, :, pl.ds(q, q)], weight_sem.at[b, 1]),
            pltpu.make_async_copy(wd_hbm.at[lay, cols, :], wdn.at[b], weight_sem.at[b, 2]),
        )

    def tile_loads(a_hbm, d_hbm, t):
        b, rows = lax.rem(t, 2), pl.ds(mult(t * tm, tm), tm)
        return (
            pltpu.make_async_copy(a_hbm.at[rows, :], tiles.at[b, 0], tile_sem.at[b, 0]),
            pltpu.make_async_copy(d_hbm.at[rows, :], tiles.at[b, 1], tile_sem.at[b, 1]),
        )

    def start_tile(layer_1, t):
        @pl.when(layer_1)
        def _():
            for c in tile_loads(a1_hbm, dy_hbm, t):
                c.start()

        @pl.when(jnp.logical_not(layer_1))
        def _():
            for c in tile_loads(a0_hbm, dh_hbm, t):
                c.start()

    def compute(b, wb, t, layer_1):
        a, dh = tiles[b, 0], tiles[b, 1]
        at[...] = a.T
        dht[...] = dh.T
        gu = dot(a, wgu[wb])
        dact = dot(dh, wdt[...]).astype(BF16).astype(F32)
        gate, up = gu[:, :q], gu[:, q:]
        s = jax.nn.sigmoid(gate)
        silu = gate * s
        act = (silu * up).astype(BF16)
        dup = (dact * silu).astype(BF16)
        dgate = (dact * up * (s + silu * (1 - s))).astype(BF16)
        dgu = jnp.concatenate([dgate, dup], -1)
        accgu[...] += dot(at[...], dgu)
        accd[...] += dot(dht[...], act)
        if layer_1:
            rows = pl.ds(mult(t * tm, tm), tm)
            da[rows, :] += dot(dgu, wgut[...])

    def between_layers():
        def loads(t):
            return tile_loads(h1_hbm, dy_hbm, t)

        def store(t):
            return pltpu.make_async_copy(hout.at[lax.rem(t, 2)], dh_hbm.at[pl.ds(mult(t * tm, tm), tm), :], hout_sem.at[lax.rem(t, 2)])

        for c in loads(0):
            c.start()

        def tile(t, _):
            @pl.when(t + 1 < steps)
            def _():
                for c in loads(t + 1):
                    c.start()

            for c in loads(t):
                c.wait()

            @pl.when(t >= 2)
            def _():
                store(t - 2).wait()

            b = lax.rem(t, 2)
            g = da[pl.ds(mult(t * tm, tm), tm), :].astype(BF16).astype(F32)
            wide = tiles[b, 0].astype(F32)
            scale = norm_scale(wide)
            inner = jnp.mean(g * wide, -1, keepdims=True)
            hout[b] = tiles[b, 1] + (scale * g - wide * (scale * scale * scale * inner)).astype(BF16)
            store(t).start()
            return 0

        lax.fori_loop(0, steps, tile, 0)
        store(steps - 2).wait()
        store(steps - 1).wait()

    for c in weight_loads(0):
        c.start()
    start_tile(True, 0)
    da[...] = jnp.zeros_like(da)

    def block(it, _):
        layer_1 = it < blocks
        wb, i = lax.rem(it, 2), lax.rem(it, blocks)
        ends_group = (i == 3) | (i == 7) | (i == blocks - 1)
        after_group = (i == 4) | (i == 8) | (it == blocks)
        p = PACKS * (it // blocks) + i + 2 * (i // 4)
        before = it - 1
        bi = lax.rem(before + blocks, blocks)
        prev = PACKS * (before // blocks) + bi + 2 * (bi // 4)

        @pl.when(it == blocks)
        def _():
            between_layers()
            start_tile(False, 0)

        for c in weight_loads(it):
            c.wait()

        @pl.when(it + 1 < 2 * blocks)
        def _():
            for c in weight_loads(it + 1):
                c.start()

        wdt[...] = wdn[wb].T

        @pl.when(layer_1)
        def _():
            wgut[...] = wgu[wb].T

        accgu[...] = jnp.zeros_like(accgu)
        accd[...] = jnp.zeros_like(accd)

        def tile(t, _):
            b = lax.rem(t, 2)
            for c in tile_loads(a1_hbm, dy_hbm, t):
                c.wait()

            more = (t + 1 < steps) | ((it + 1 != blocks) & (it + 1 != 2 * blocks))

            @pl.when(more)
            def _():
                start_tile(layer_1, lax.rem(t + 1, steps))

            @pl.when(layer_1)
            def _():
                compute(b, wb, t, True)

            @pl.when(jnp.logical_not(layer_1))
            def _():
                compute(b, wb, t, False)

            @pl.when((t == 1) & (it >= 1))
            def _():
                half(prev)

                @pl.when(after_group)
                def _():
                    full(prev + 1, (DOWN, LAST))

            @pl.when((t == 3) & after_group)
            def _():
                half(prev + 1)
                full(prev + 2, (DOWN, LAST))

            @pl.when((t == 5) & after_group)
            def _():
                half(prev + 2)

            return 0

        lax.fori_loop(0, steps, tile, 0)
        k = lax.rem(i, 4)
        for c in range(d // q):
            dbuf[pl.ds(mult(k * q, q), q), c * q : (c + 1) * q] = accd[c * q : (c + 1) * q, :].astype(BF16).T
        full(p, (GU,))
        return 0

    lax.fori_loop(0, 2 * blocks, block, 0)
    end = 2 * PACKS

    def tail(p, _):
        half(p)
        full(p + 1, (DOWN, LAST))
        return 0

    lax.fori_loop(end - 3, end, tail, 0)

    def drain(p, _):
        each(do_s4, p - 2)
        each(do_s5, p - 4)
        return 0

    lax.fori_loop(end, end + 4, drain, 0)
    for p in (end - 2, end - 1):
        moment_stores_wait(LAST, p)


def backward(a1, dy, h1, a0, wg, wu, wd, moments, n, axis, tm=None):
    tm = tm or TM
    t, d = dy.shape
    ff = wg.shape[-1]
    q = BLOCK
    V = pltpu.VMEM
    DMA = pltpu.SemaphoreType.DMA
    mg, mu, md, vg, vu, vd = moments
    outs = [jax.ShapeDtypeStruct(w.shape, BF16) for w in (wg, wu, wd)]
    outs += [jax.ShapeDtypeStruct(m.shape, F32) for m in moments]
    outs += [jax.ShapeDtypeStruct((t, d), BF16)]
    return pl.pallas_call(
        functools.partial(backward_kernel, n, t // tm, d, ff, axis),
        in_specs=[ANY] * 13,
        out_specs=[ANY] * 10,
        out_shape=outs,
        scratch_shapes=[
            V((2, 2, tm, d), BF16),
            V((d, tm), BF16),
            V((d, tm), BF16),
            V((2, d, 2 * q), BF16),
            V((2, q, d), BF16),
            V((d, q), BF16),
            V((2 * q, d), BF16),
            V((d, 2 * q), F32),
            V((d, q), F32),
            V((t, d), F32),
            V((4 * q, d), BF16),
            V((2, tm, d), BF16),
            V((RING, 2, 2 * q, q), BF16),
            V((RING, 2, q, q), BF16),
            V((RING, 2, q, q), BF16),
            V((RING, 2, 2 * q, q), BF16),
            V((RING, 2, q, q), BF16),
            V((RING, 2, q, q), BF16),
            V((RING, 2, q, q), BF16),
            V((2, 4, q, q), F32),
            V((2, 2, q, q), BF16),
            V((2, 4, q, q), F32),
            DMA((2, 2)),
            DMA((2, 3)),
            DMA((2,)),
            DMA((2, RING)),
            DMA((2, RING)),
            DMA((2, RING)),
            DMA((2, RING)),
            DMA((2, 2, RING)),
            DMA((2, 2, RING)),
            DMA((2, 2 * RING)),
            DMA((2, 2 * RING)),
            DMA((2, RING)),
            DMA((2, 6)),
            DMA((2, 4)),
        ],
        compiler_params=pltpu.CompilerParams(vmem_limit_bytes=62 * MIB, collective_id=0, has_side_effects=True),
        cost_estimate=pl.CostEstimate(flops=28 * t * d * ff, bytes_accessed=44 * t * d, transcendentals=2 * t * ff),
        name="backward",
    )(a1, dy, h1, a0, wg, wu, wd, *moments)


def solution(mesh):
    n = mesh.shape["dp"]

    def step(x, dy, wg, wu, wd, m_g, m_u, m_d, v_g, v_u, v_d):
        x, dy = x[0], dy[0]
        a0, h1, a1 = forward(x, wg, wu, wd)
        return backward(a1, dy, h1, a0, wg, wu, wd, (m_g, m_u, m_d, v_g, v_u, v_d), n, "dp")[:9]

    seq = P(("rep", "dp"), None, None)
    rows = P(None, "dp", None)
    whole = P("rep", None, None)
    part = P("rep", "dp", None)
    return jax.shard_map(
        step,
        mesh=mesh,
        in_specs=(seq, seq, P(), P(), P()) + (rows,) * 6,
        out_specs=(whole,) * 3 + (part,) * 6,
        check_vma=False,
    )
```

time: 1420 us -> 858 us (0.60)
  Pallas kernels: 0 us -> 809 us
  waiting for transfers between devices: 677 us -> 0 us
  matrix products: 526 us -> 0 us
  other arithmetic: 142 us -> 0.01 us
  between operations: 15.2 us -> 0.74 us
    pallas_call x0 -> x2, Pallas kernels: none -> 809 us  [the longest x1 723 us: backward(): pl.pallas_call(functools.partial(backward_kernel, n, t // tm, d, ff, axis...]
    dot_general x15 -> x0, matrix products: 526 us -> none  [the longest x5 177 us: layer(): up = jnp.dot(a, w['w_up'], preferred_element_type=jnp.float32)]
    unnamed x15 -> x0, waiting for transfers between devices: 363 us -> none
    reshape x3 -> x0, waiting for transfers between devices: 314 us -> none  [step(): t.reshape(-1, *t.shape[2:])]
    unnamed x6 -> x7, other arithmetic: 95.2 us -> 0.01 us
    reshape x3 -> x0, other arithmetic: 29.6 us -> none  [step(): t.reshape(-1, *t.shape[2:])]
  transfers between devices with their start and end apart: 9 -> 0, of which waited for: 7 -> 0; matrix products, arithmetic and copies ran while one was open for 19% -> 0% of each run, Pallas kernels for 0% -> 0%
where the time goes in v1:
time: 858 us; the launch traced here: 857 us
  Pallas kernels  809 us (94%)
  local copies, waits for them, and re-layouts  47.9 us (6%)
    pallas_call x1, Pallas kernels, backward(): pl.pallas_call(functools.partial(backward_kernel, n, t // tm, d, ff, axis...  723 us
    pallas_call x1, Pallas kernels, forward(): pl.pallas_call(functools.partial(forward_kernel, blocks), grid=(t // tm,)...  85.7 us
    unnamed x41, local copies, waits for them, and re-layouts  47.9 us

profile of v1, /device:TPU:112, one launch (start us, length us, event | category | flops | bytes accessed | tf_op | source)
XLA Modules:
  0.0 857.4 jit_solution(18151889625863483442)
XLA Ops:
  0.6 85.7 %forward.1 = (bf16[4096,1024]{1,0:T(8,128)(2,1)}, bf16[4096,1024]{1,0:T(8,128)(2,1)}, bf16[4096,1024]{1,0:T(8,128)(2,1)}) custom-call(bf16[4096,1024]{1,0:T(8,128)(2,1)} %bitcast.16, bf16[2,1024,2816]{2,1,0:T(8,128)(2,1)} %wg_hbm.3, bf16[2,1024,2816]{2,1,0:T(8,128)(2,1)} %wu_hbm.3, bf16[2,2816,1024]{2,1,0:T(8,128)(2,1)} %wd_hbm.3), custom_call_target="tpu_custom_call" | custom-call | flops 70866960384 | bytes 50855936 | tf_op jit(solution)/shard_map/forward/pallas_call | solution.py:73
  86.3 723.0 %backward.1 = (bf16[2,1024,2816]{2,1,0:T(8,128)(2,1)}, bf16[2,1024,2816]{2,1,0:T(8,128)(2,1)}, bf16[2,2816,1024]{2,1,0:T(8,128)(2,1)}, f32[2,256,2816]{2,1,0:T(8...) custom-call(bf16[4096,1024]{1,0:T(8,128)(2,1)} %get-tuple-element.21, ...), custom_call_target="tpu_custom_call" | custom-call | flops 330712481792 | bytes 184549376 | tf_op jit(solution)/shard_map/backward/pallas_call | solution.py:543
  809.4 0.0 copy-start
  809.4 0.0 slice-start
  809.4 0.0 slice-start.1
  809.4 11.7 %copy.29 = bf16[2,1024,2816]{2,1,0:T(8,128)(2,1)} copy(bf16[2,1024,2816]{2,1,0:T(8,128)(2,1)} %get-tuple-element.42) | data formatting | bytes 23068672
  821.1 0.0 copy-done
  821.1 0.0 slice-start.11
  821.1 0.0 slice-start.9
  821.1 5.8 copy.30
  827.0 0.0 slice-done
  827.0 0.6 slice-done.1
  827.6 1.4 slice-done.2
  829.0 5.8 copy.31
  834.8 0.0 slice-done.13
  834.8 2.4 slice-done.14
  837.2 2.5 copy.32
  839.7 0.0 slice-done.11
  839.7 0.0 slice-done.12
  839.7 0.0 slice-start.5
  839.7 2.9 copy.33
  842.7 0.0 slice-done.9
  842.7 0.0 slice-done.10
  842.7 0.0 slice-start.6
  842.7 2.9 copy.34
  845.6 0.0 slice-done.7
  845.6 2.3 slice-done.8
  848.0 2.9 copy.35
  850.9 0.0 slice-done.5
  850.9 2.9 copy.36
  853.8 1.1 slice-done.4
  854.9 2.5 copy.37
  (18 shorter events, 0.0 us)
Async XLA Ops:
  809.4 11.7 %copy-start = (bf16[2,1024,2816]{2,1,0:T(8,128)(2,1)S(1)}, bf16[2,1024,2816]{2,1,0:T(8,128)(2,1)}, u32[]{:S(2)}) copy-start(bf16[2,1024,2816]{2,1,0:T(8,128)(2,1)} %get-tuple-element.43) | copy-start | bytes 34603012
  809.4 17.6 %slice-start = ((s8[11534336]{0:T(1024)(128)(4,1)}), s8[4194304]{0:T(1024)(128)(4,1)S(1)}, s32[]{:S(2)}) async-start(s8[11534336]{0:T(1024)(128)(4,1)} %bitcast.2), calls=%async_computation | async-start | bytes 8388608
  809.4 18.1 %slice-start.1 = ((s8[11534336]{0:T(1024)(128)(4,1)}), s8[4194304]{0:T(1024)(128)(4,1)S(1)}, s32[]{:S(2)}) async-start(s8[11534336]{0:T(1024)(128)(4,1)} %bitcast.2), calls=%async_computation.1 | async-start | bytes 8388608
  821.1 7.8 slice-start.2
  821.1 13.7 %slice-start.13 = ((s8[5767168]{0:T(1024)(128)(4,1)}), s8[1572864]{0:T(1024)(128)(4,1)S(1)}, s32[]{:S(2)}) async-start(s8[5767168]{0:T(1024)(128)(4,1)} %bitcast.14), calls=%async_computation.13 | async-start | bytes 3145728
  821.1 18.6 %slice-start.11 = ((s8[5767168]{0:T(1024)(128)(4,1)}), s8[4194304]{0:T(1024)(128)(4,1)S(1)}, s32[]{:S(2)}) async-start(s8[5767168]{0:T(1024)(128)(4,1)} %bitcast.12), calls=%async_computation.11 | async-start | bytes 8388608
  821.1 21.5 %slice-start.9 = ((s8[5767168]{0:T(1024)(128)(4,1)}), s8[4194304]{0:T(1024)(128)(4,1)S(1)}, s32[]{:S(2)}) async-start(s8[5767168]{0:T(1024)(128)(4,1)} %bitcast.10), calls=%async_computation.9 | async-start | bytes 8388608
  829.0 8.2 slice-start.14
  829.0 10.8 %slice-start.12 = ((s8[5767168]{0:T(1024)(128)(4,1)}), s8[1572864]{0:T(1024)(128)(4,1)S(1)}, s32[]{:S(2)}) async-start(s8[5767168]{0:T(1024)(128)(4,1)} %bitcast.12), calls=%async_computation.12 | async-start | bytes 3145728
  829.0 13.7 %slice-start.10 = ((s8[5767168]{0:T(1024)(128)(4,1)}), s8[1572864]{0:T(1024)(128)(4,1)S(1)}, s32[]{:S(2)}) async-start(s8[5767168]{0:T(1024)(128)(4,1)} %bitcast.10), calls=%async_computation.10 | async-start | bytes 3145728
  839.7 5.9 slice-start.7
  839.7 11.2 %slice-start.5 = ((s8[5767168]{0:T(1024)(128)(4,1)}), s8[4194304]{0:T(1024)(128)(4,1)S(1)}, s32[]{:S(2)}) async-start(s8[5767168]{0:T(1024)(128)(4,1)} %bitcast.6), calls=%async_computation.5 | async-start | bytes 8388608
  842.7 5.3 slice-start.8
  842.7 8.2 slice-start.6
  848.0 5.8 slice-start.3
  850.9 4.0 slice-start.4

commit v2 on v1

--- a/solution.py
+++ b/solution.py
@@ -97,27 +97,45 @@
 
 
 GU, DOWN, LAST = 0, 1, 2
-RING = 4
-PACKS = 17
-
-
-def pack_kind(p):
-    r = lax.rem(p, PACKS)
-    down = ((r >= 4) & (r < 6)) | ((r >= 10) & (r < 12))
-    last = r >= 15
-    return {GU: jnp.logical_not(down | last), DOWN: down, LAST: last}
+RING = 6
+LEAD = 4
+QUARTERS = 4
+GROUPS = 3
+KEPT = 11
+SLOTS = 12
+AHEAD = 6
+
+
+def pack_of_block(it):
+    return jnp.where(it < LEAD, it, 2 * it - LEAD + 1)
+
+
+def pack_kind(p, blocks):
+    paired = (p >= LEAD) & (p < 4 * blocks - LEAD)
+    down = (paired & (lax.rem(p, 2) == 0)) | (p >= 4 * blocks - LEAD)
+    last = down & (lax.rem(pack_down(p, blocks) // QUARTERS, GROUPS) == GROUPS - 1)
+    return {GU: jnp.logical_not(down), DOWN: down & jnp.logical_not(last), LAST: last}
+
+
+def pack_block(p):
+    return jnp.where(p < LEAD, p, (p + LEAD - 1) // 2)
+
+
+def pack_down(p, blocks):
+    return jnp.where(p < 4 * blocks - LEAD, jnp.maximum(p - LEAD, 0) // 2, p - 2 * blocks)
 
 
 def backward_kernel(
     n, steps, d, ff, axis,
     a1_hbm, dy_hbm, h1_hbm, a0_hbm, wg_hbm, wu_hbm, wd_hbm, mg_hbm, mu_hbm, md_hbm, vg_hbm, vu_hbm, vd_hbm,
-    ng_hbm, nu_hbm, nd_hbm, mg_out, mu_out, md_out, vg_out, vu_out, vd_out, dh_hbm,
+    ng_hbm, nu_hbm, nd_hbm, mg_out, mu_out, md_out, vg_out, vu_out, vd_out, dh_hbm, kept_a, kept_b,
     tiles, at, dht, wgu, wdn, wdt, wgut, accgu, accd, da, dbuf, hout,
     send, keep, own, r1, r2, s2, wnew, mvin, win, mvout,
     tile_sem, weight_sem, hout_sem, s1s, s1r, s2s, s2r, g1s, g1r, g2s, g2r, loc_sem, mvin_sem, mvout_sem,
 ):
     tm = tiles.shape[2]
     blocks = ff // BLOCK
+    packs = 2 * blocks + 2 * GROUPS * QUARTERS
     q = BLOCK
     me = lax.axis_index(axis)
     right, left, far = (lax.rem(me + k, n) for k in (1, n - 1, 2))
@@ -130,39 +148,50 @@
     pl.semaphore_wait(barrier, 2)
 
 
-    def layer_of(p):
-        return 1 - p // PACKS
-
-    def gu_cols(p):
-        r = lax.rem(p, PACKS)
-        i = jnp.where(r < 4, r, jnp.where(r < 10, r - 2, r - 4))
+    kind_of = functools.partial(pack_kind, blocks=blocks)
+
+    def block_cols(it):
+        i = lax.rem(it, blocks)
         return mult((3 * lax.rem(i, 4) + i // 4) * q, q)
 
-    def down_cols(kind, p, half):
-        r = lax.rem(p, PACKS)
-        first = r - 15 if kind == LAST else jnp.where(r < 6, r - 4, r - 10)
-        return mult((2 * first + half) * q, q)
-
-    def down_row(p, dev):
-        r = lax.rem(p, PACKS)
-        return mult(jnp.where(r < 6, 0, 4 * UNIT) + dev * UNIT, UNIT)
-
-    def last_row(dev, u):
-        return mult(jnp.where(u < dev, u, 8 + u) * UNIT, UNIT)
+    def down_group(p):
+        return pack_down(p, blocks) // QUARTERS
+
+    def down_cols(p):
+        return mult(lax.rem(pack_down(p, blocks), QUARTERS) * q, q)
 
     def height(kind):
-        return 3 * UNIT if kind == LAST else q
+        return {GU: q, DOWN: q // 2, LAST: 3 * UNIT // 2}[kind]
+
+    def last_row(dev, k):
+        u = k // 2
+        return mult(jnp.where(u < dev, u * UNIT, 8 * UNIT + u * UNIT) + (k % 2) * (UNIT // 2), UNIT // 2)
 
     def rows_in(kind, p, dev, half, ref_gu, ref_d, per_device):
-        lay = layer_of(p)
         if kind == GU:
+            it = pack_block(p)
             base = 0 if per_device else mult(dev * q, q)
-            return [(ref_gu[half].at[lay, pl.ds(base, q), pl.ds(gu_cols(p), q)], 0, q)]
-        cols = pl.ds(down_cols(kind, p, half), q)
+            return [(ref_gu[half].at[1 - it // blocks, pl.ds(base, q), pl.ds(block_cols(it), q)], 0, q)]
+        group = down_group(p)
+        lay, cols = 1 - group // GROUPS, pl.ds(down_cols(p), q)
         base = 0 if per_device else dev * (ff // n)
         if kind == DOWN:
-            return [(ref_d.at[lay, pl.ds(mult(base + down_row(p, dev), UNIT), q), cols], 0, q)]
-        return [(ref_d.at[lay, pl.ds(mult(base + last_row(dev, u), UNIT), UNIT), cols], u * UNIT, UNIT) for u in range(3)]
+            row = base + lax.rem(group, GROUPS) * 4 * UNIT + dev * UNIT + half * (q // 2)
+            return [(ref_d.at[lay, pl.ds(mult(row, UNIT), q // 2), cols], 0, q // 2)]
+        small = UNIT // 2
+        return [
+            (ref_d.at[lay, pl.ds(mult(base + last_row(dev, 3 * half + k), small), small), cols], k * small, small) for k in range(3)
+        ]
+
+    def kept_rows(kind, p):
+        k = p - (packs - KEPT)
+        pair, small = q + q // 2, 3 * UNIT // 2
+        row = {
+            GU: k // 2 * pair,
+            DOWN: jnp.where(k < 5, k // 2 * pair + q, 2 * pair + q + (k - 5) * (q // 2)),
+            LAST: 3 * pair + q // 2 + (k - 7) * small,
+        }[kind]
+        return pl.ds(mult(row, UNIT // 2), height(kind))
 
     def new_pieces(kind, p, dev, half):
         return rows_in(kind, p, dev, half, (ng_hbm, nu_hbm), nd_hbm, False)
@@ -242,14 +271,25 @@
             for view, at_, size in new_pieces(kind, p, me, half)
         ]
 
+    def kept_copies(kind, p):
+        s, h = lax.rem(p, RING), height(kind)
+        return [
+            pltpu.make_async_copy(wnew.at[s, half, pl.ds(0, h)], (kept_a, kept_b)[half].at[kept_rows(kind, p)], loc_sem.at[half, s]) for half in range(2)
+        ]
+
+    def leaves(p):
+        return p < packs - KEPT
+
     def stage(kind, p):
         s, h = lax.rem(p, RING), height(kind)
         if kind == GU:
             def part(dev, half):
                 return accgu[pl.ds(mult(dev * q, q), q), half * q : (half + 1) * q].astype(BF16)
         else:
+            slot = lax.rem(down_group(p), 2)
+
             def part(dev, half):
-                return dbuf[pl.ds(mult(dev * h, UNIT), h), pl.ds(down_cols(kind, p, half), q)]
+                return dbuf[slot, pl.ds(mult(dev * (2 * h) + half * h, UNIT // 2), h), pl.ds(down_cols(p), q)]
         send[s, 0, :h, :] = part(far, 0)
         send[s, 0, h : 2 * h, :] = part(right, 1)
         send[s, 1, :h, :] = part(far, 1)
@@ -261,13 +301,13 @@
 
     def do_s1(kind, p):
         stage(kind, p)
+        for way in range(2):
+            s1_copy(kind, p, way).start()
+
+    def do_s2(kind, p):
+        s, h = lax.rem(p, RING), height(kind)
         for c in moment_loads(kind, p):
             c.start()
-        for way in range(2):
-            s1_copy(kind, p, way).start()
-
-    def do_s2(kind, p):
-        s, h = lax.rem(p, RING), height(kind)
         for way in range(2):
             s1_copy(kind, p, way).wait_recv()
             s2[s, way, :h, :] = (keep[s, way, :h, :].astype(F32) + r1[s, way, :h, :].astype(F32)).astype(BF16)
@@ -276,7 +316,7 @@
     def do_s3(kind, p):
         s, b, h = lax.rem(p, RING), lax.rem(p, 2), height(kind)
         moment_loads_wait(kind, p)
-        for k, cond in pack_kind(p - 2).items():
+        for k, cond in kind_of(p - 2).items():
             @pl.when(cond & (p >= 2))
             def _():
                 moment_stores_wait(k, p - 2)
@@ -284,8 +324,8 @@
             s2_copy(kind, p, way).wait_recv()
 
         def rows_of(u, _):
-            rows = pl.ds(mult(u * UNIT, UNIT), UNIT)
-            rest = pl.ds(mult(h + u * UNIT, UNIT), UNIT)
+            rows = pl.ds(mult(u * (UNIT // 2), UNIT // 2), UNIT // 2)
+            rest = pl.ds(mult(h + u * (UNIT // 2), UNIT // 2), UNIT // 2)
             for half in range(2):
                 g = own[s, half, rows, :].astype(F32) + r1[s, 1 - half, rest, :].astype(F32) + r2[s, half, rows, :].astype(F32)
                 g = g.astype(BF16).astype(F32)
@@ -295,59 +335,80 @@
                 mvout[b, 2 * half + 1, rows, :] = v
             return 0
 
-        lax.fori_loop(0, h // UNIT, rows_of, 0)
+        lax.fori_loop(0, h // (UNIT // 2), rows_of, 0)
         for c in moment_stores(kind, p):
             c.start()
-        for way in range(2):
-            for half in ((0, 1), (1, 0))[way]:
-                for c in g1_copies(kind, p, way, half):
-                    c.start()
-        for c in own_copies(kind, p):
-            c.start()
+
+        @pl.when(leaves(p))
+        def _():
+            for way in range(2):
+                for half in ((0, 1), (1, 0))[way]:
+                    for c in g1_copies(kind, p, way, half):
+                        c.start()
+            for c in own_copies(kind, p):
+                c.start()
+
+        @pl.when(jnp.logical_not(leaves(p)))
+        def _():
+            for c in kept_copies(kind, p):
+                c.start()
 
     def do_s4(kind, p):
         s = lax.rem(p, RING)
         for way in range(2):
             s1_copy(kind, p, way).wait_send()
             s2_copy(kind, p, way).wait_send()
-            for half in ((0, 1), (1, 0))[way]:
-                total_of(kind, p, way, half, (g1s.at[way, half, s], g1r.at[way, half, s]), 1)
-                if half == way:
-                    for c in g2_copies(kind, p, way):
-                        c.start()
+
+        @pl.when(leaves(p))
+        def _():
+            for way in range(2):
+                for half in ((0, 1), (1, 0))[way]:
+                    total_of(kind, p, way, half, (g1s.at[way, half, s], g1r.at[way, half, s]), 1)
+                    if half == way:
+                        for c in g2_copies(kind, p, way):
+                            c.start()
 
     def do_s5(kind, p):
         s, rows = lax.rem(p, RING), pl.ds(0, height(kind))
-        for way in range(2):
-            for half in range(2):
-                total_of(kind, p, way, half, (g1s.at[way, half, s], g1r.at[way, half, s]), 0)
-            far_s = lax.rem(p, 2 * RING)
-            total_of(kind, p, way, way, (g2s.at[way, far_s], g2r.at[way, far_s]), 1)
-            total_of(kind, p, way, way, (g2s.at[way, far_s], g2r.at[way, far_s]), 0)
+        far_s = lax.rem(p, 2 * RING)
+
+        @pl.when(leaves(p))
+        def _():
+            for way in range(2):
+                for half in range(2):
+                    total_of(kind, p, way, half, (g1s.at[way, half, s], g1r.at[way, half, s]), 0)
+                total_of(kind, p, way, way, (g2s.at[way, far_s], g2r.at[way, far_s]), 1)
+                total_of(kind, p, way, way, (g2s.at[way, far_s], g2r.at[way, far_s]), 0)
+
         for half in range(2):
             pltpu.make_async_copy(wnew.at[s, half, rows], wnew.at[s, half, rows], loc_sem.at[half, s]).wait()
 
     def each(do, p, among=(GU, DOWN, LAST)):
-        for kind, cond in pack_kind(p).items():
+        for kind, cond in kind_of(p).items():
             if kind in among:
-                @pl.when(cond & (p >= 0) & (p < 2 * PACKS))
+                @pl.when(cond & (p >= 0) & (p < packs))
                 def _():
                     do(kind, p)
 
+    deep = LEAD + 1
+
+    def lagged(do, p, first, among=(GU, DOWN, LAST)):
+        early = p - first < deep
+        each(do, jnp.where(early, p - first, jnp.where(p - first == deep, -1, p - first - 1)), among)
+
     def full(p, among=(GU, DOWN, LAST)):
         each(do_s1, p, among)
-        each(do_s3, p - 1)
+        lagged(do_s3, p, 1)
 
     def half(p):
-        each(do_s2, p)
-        each(do_s4, p - 2)
-        each(do_s5, p - 4)
+        lagged(do_s2, p, 0)
+        lagged(do_s4, p, 2)
+        each(do_s5, p - 5)
 
 
     def weight_loads(it):
         b, lay = lax.rem(it, 2), 1 - it // blocks
-        i = lax.rem(it, blocks)
-        cols = pl.ds(mult((3 * lax.rem(i, 4) + i // 4) * q, q), q)
+        cols = pl.ds(block_cols(it), q)
         return (
             pltpu.make_async_copy(wg_hbm.at[lay, :, cols], wgu.at[b, :, pl.ds(0, q)], weight_sem.at[b, 0]),
             pltpu.make_async_copy(wu_hbm.at[lay, :, cols], wgu.at[b, :, pl.ds(q, q)], weight_sem.at[b, 1]),
@@ -374,22 +435,26 @@
 
     def compute(b, wb, t, layer_1):
         a, dh = tiles[b, 0], tiles[b, 1]
+        m = tm // 2
         at[...] = a.T
         dht[...] = dh.T
-        gu = dot(a, wgu[wb])
-        dact = dot(dh, wdt[...]).astype(BF16).astype(F32)
-        gate, up = gu[:, :q], gu[:, q:]
-        s = jax.nn.sigmoid(gate)
-        silu = gate * s
-        act = (silu * up).astype(BF16)
-        dup = (dact * silu).astype(BF16)
-        dgate = (dact * up * (s + silu * (1 - s))).astype(BF16)
-        dgu = jnp.concatenate([dgate, dup], -1)
-        accgu[...] += dot(at[...], dgu)
-        accd[...] += dot(dht[...], act)
-        if layer_1:
-            rows = pl.ds(mult(t * tm, tm), tm)
-            da[rows, :] += dot(dgu, wgut[...])
+        dact = [dot(dh[r], wdt[...]) for r in (slice(0, m), slice(m, tm))]
+        gu = [dot(a[r], wgu[wb]) for r in (slice(0, m), slice(m, tm))]
+        for k in range(2):
+            rows = slice(k * m, (k + 1) * m)
+            gate, up = gu[k][:, :q], gu[k][:, q:]
+            dk = dact[k].astype(BF16).astype(F32)
+            s = jax.nn.sigmoid(gate)
+            silu = gate * s
+            act = (silu * up).astype(BF16)
+            dup = (dk * silu).astype(BF16)
+            dgate = (dk * up * (s + silu * (1 - s))).astype(BF16)
+            dgu = jnp.concatenate([dgate, dup], -1)
+            if layer_1:
+                da[pl.ds(mult(t * tm + k * m, m), m), :] += dot(dgu, wgut[...])
+            accgu[...] += dot(at[:, rows], dgu)
+            for r in (slice(0, d // 2), slice(d // 2, d)):
+                accd[r, :] += dot(dht[r, rows], act)
 
     def between_layers():
         def loads(t):
@@ -435,12 +500,8 @@
     def block(it, _):
         layer_1 = it < blocks
         wb, i = lax.rem(it, 2), lax.rem(it, blocks)
-        ends_group = (i == 3) | (i == 7) | (i == blocks - 1)
-        after_group = (i == 4) | (i == 8) | (it == blocks)
-        p = PACKS * (it // blocks) + i + 2 * (i // 4)
-        before = it - 1
-        bi = lax.rem(before + blocks, blocks)
-        prev = PACKS * (before // blocks) + bi + 2 * (bi // 4)
+        p = pack_of_block(it)
+        with_down = it >= LEAD
 
         @pl.when(it == blocks)
         def _():
@@ -485,46 +546,34 @@
 
             @pl.when((t == 1) & (it >= 1))
             def _():
-                half(prev)
-
-                @pl.when(after_group)
-                def _():
-                    full(prev + 1, (DOWN, LAST))
-
-            @pl.when((t == 3) & after_group)
-            def _():
-                half(prev + 1)
-                full(prev + 2, (DOWN, LAST))
-
-            @pl.when((t == 5) & after_group)
-            def _():
-                half(prev + 2)
+                half(pack_of_block(it - 1))
+
+            @pl.when((t == 3) & with_down)
+            def _():
+                full(p - 1, (DOWN, LAST))
+
+            @pl.when((t == 5) & with_down)
+            def _():
+                half(p - 1)
 
             return 0
 
         lax.fori_loop(0, steps, tile, 0)
-        k = lax.rem(i, 4)
+        k, slot = lax.rem(i, 4), lax.rem(i // 4 + jnp.where(layer_1, 0, 1), 2)
         for c in range(d // q):
-            dbuf[pl.ds(mult(k * q, q), q), c * q : (c + 1) * q] = accd[c * q : (c + 1) * q, :].astype(BF16).T
+            dbuf[slot, pl.ds(mult(k * q, q), q), c * q : (c + 1) * q] = accd[c * q : (c + 1) * q, :].astype(BF16).T
         full(p, (GU,))
         return 0
 
     lax.fori_loop(0, 2 * blocks, block, 0)
-    end = 2 * PACKS
+    end = packs
 
     def tail(p, _):
         half(p)
         full(p + 1, (DOWN, LAST))
         return 0
 
-    lax.fori_loop(end - 3, end, tail, 0)
-
-    def drain(p, _):
-        each(do_s4, p - 2)
-        each(do_s5, p - 4)
-        return 0
-
-    lax.fori_loop(end, end + 4, drain, 0)
+    lax.fori_loop(4 * blocks - LEAD - 1, end + 5, tail, 0)
     for p in (end - 2, end - 1):
         moment_stores_wait(LAST, p)
 
@@ -539,11 +588,11 @@
     mg, mu, md, vg, vu, vd = moments
     outs = [jax.ShapeDtypeStruct(w.shape, BF16) for w in (wg, wu, wd)]
     outs += [jax.ShapeDtypeStruct(m.shape, F32) for m in moments]
-    outs += [jax.ShapeDtypeStruct((t, d), BF16)]
+    outs += [jax.ShapeDtypeStruct((t, d), BF16), *[jax.ShapeDtypeStruct((kept_height(), q), BF16)] * 2]
     return pl.pallas_call(
         functools.partial(backward_kernel, n, t // tm, d, ff, axis),
         in_specs=[ANY] * 13,
-        out_specs=[ANY] * 10,
+        out_specs=[ANY] * 12,
         out_shape=outs,
         scratch_shapes=[
             V((2, 2, tm, d), BF16),
@@ -556,7 +605,7 @@
             V((d, 2 * q), F32),
             V((d, q), F32),
             V((t, d), F32),
-            V((4 * q, d), BF16),
+            V((2, 4 * q, d), BF16),
             V((2, tm, d), BF16),
             V((RING, 2, 2 * q, q), BF16),
             V((RING, 2, q, q), BF16),
@@ -589,13 +638,148 @@
     )(a1, dy, h1, a0, wg, wu, wd, *moments)
 
 
+def kept_height():
+    return 3 * BLOCK + 4 * (BLOCK // 2) + 4 * (3 * UNIT // 2)
+
+
+def results_kernel(count, rows, *refs):
+    sources, rest = refs[:count], refs[count + 1 :]
+    outs, rest = rest[:count], rest[count:]
+    kinds = []
+    for r in sources:
+        if (key := (r.shape[1:], r.dtype)) not in kinds:
+            kinds.append(key)
+    buffers, (isem, osem) = rest[: len(kinds)], rest[len(kinds) :]
+    steps, used = [], [0] * len(kinds)
+    for k, r in enumerate(sources):
+        kind = kinds.index((r.shape[1:], r.dtype))
+        size = buffers[kind].shape[1]
+        for lay in range(r.shape[0]):
+            for at_ in range(0, r.shape[1], size):
+                steps.append((k, kind, used[kind] % SLOTS, lay, at_, size))
+                used[kind] += 1
+
+    def copy_in(step):
+        k, kind, slot, lay, at_, size = steps[step]
+        return pltpu.make_async_copy(sources[k].at[lay, pl.ds(at_, size)], buffers[kind].at[slot], isem.at[kind, slot])
+
+    def copy_out(step):
+        k, kind, slot, lay, at_, size = steps[step]
+        return pltpu.make_async_copy(buffers[kind].at[slot], outs[k].at[lay, pl.ds(at_, size)], osem.at[kind, slot])
+
+    flying = {}
+
+    def start_in(step):
+        key = steps[step][1:3]
+        if key in flying:
+            copy_out(flying.pop(key)).wait()
+        copy_in(step).start()
+
+    for step in range(min(AHEAD, len(steps))):
+        start_in(step)
+    for step in range(len(steps)):
+        copy_in(step).wait()
+        copy_out(step).start()
+        flying[steps[step][1:3]] = step
+        if step + AHEAD < len(steps):
+            start_in(step + AHEAD)
+    for step in flying.values():
+        copy_out(step).wait()
+
+
+def results(sources, token):
+    piece = 128 * 2816 * 2
+    kinds = []
+    for r in sources:
+        if (key := (r.shape[1:], r.dtype)) not in kinds:
+            kinds.append(key)
+    buffers = []
+    for (_, width), dtype in kinds:
+        buffers.append(pltpu.VMEM((SLOTS, piece // (width * dtype.itemsize), width), dtype))
+    size = sum(r.size * r.dtype.itemsize for r in sources)
+    return pl.pallas_call(
+        functools.partial(results_kernel, len(sources), None),
+        in_specs=[ANY] * (len(sources) + 1),
+        out_specs=[ANY] * len(sources),
+        out_shape=[jax.ShapeDtypeStruct(r.shape, r.dtype) for r in sources],
+        scratch_shapes=buffers + [pltpu.SemaphoreType.DMA((len(kinds), SLOTS))] * 2,
+        compiler_params=pltpu.CompilerParams(vmem_limit_bytes=62 * MIB),
+        cost_estimate=pl.CostEstimate(flops=20 * 10**9, bytes_accessed=2 * size, transcendentals=0),
+        name="results",
+    )(*sources, token)
+
+
+def kept_kernel(n, axis, blocks, a, b, la, lb, ra, rb, fa, fb, ng, nu, nd, ng_out, nu_out, nd_out, sem):
+    q, u = BLOCK, UNIT
+    me = lax.axis_index(axis)
+    ff = nd_out.shape[1]
+    mult = pl.multiple_of
+    copies = []
+
+    def put(src, dst):
+        copies.append(pltpu.make_async_copy(src, dst, sem.at[len(copies)]))
+
+    def cols(b):
+        return pl.ds((3 * (b % 4) + b // 4) * q, q)
+
+    for far, halves in enumerate(((a, b), (ra, rb), (fa, fb), (la, lb))):
+        dev = lax.rem(me + far, n)
+        base = dev * (ff // n)
+        for half, src in enumerate(halves):
+            out = (ng_out, nu_out)[half]
+            rows = pl.ds(mult(dev * q, q), q)
+            pair = q + q // 2
+            for k in range(3):
+                put(src.at[pl.ds(k * pair, q)], out.at[0, rows, cols(blocks - 3 + k)])
+            for quarter, at_ in enumerate((q, pair + q, 2 * pair + q, 3 * pair)):
+                row = pl.ds(mult(base + 4 * u + dev * u + half * (q // 2), u), q // 2)
+                put(src.at[pl.ds(at_, q // 2)], nd_out.at[0, row, pl.ds(quarter * q, q)])
+            for quarter in range(4):
+                at_ = 3 * pair + q // 2 + quarter * (3 * u // 2)
+                for j in range(3):
+                    piece = 3 * half + j
+                    v = piece // 2
+                    row = base + jnp.where(v < dev, v * u, 8 * u + v * u) + (piece % 2) * (u // 2)
+                    put(src.at[pl.ds(at_ + j * (u // 2), u // 2)], nd_out.at[0, pl.ds(mult(row, u // 2), u // 2), pl.ds(quarter * q, q)])
+    for c in copies:
+        c.start()
+    for c in copies:
+        c.wait()
+
+
+def place_kept(own, parts, weights, n, axis):
+    blocks = weights[0].shape[-1] // BLOCK
+    vmem = pl.BlockSpec(memory_space=pltpu.VMEM)
+    return pl.pallas_call(
+        functools.partial(kept_kernel, n, axis, blocks),
+        in_specs=[vmem] * 8 + [ANY] * 3,
+        out_specs=[ANY] * 3,
+        out_shape=[jax.ShapeDtypeStruct(w.shape, w.dtype) for w in weights],
+        input_output_aliases={8: 0, 9: 1, 10: 2},
+        scratch_shapes=[pltpu.SemaphoreType.DMA((8 * (3 + 4 + 12),))],
+        compiler_params=pltpu.CompilerParams(vmem_limit_bytes=40 * MIB),
+        name="place_kept",
+    )(*own, *parts, *weights)
+
+
 def solution(mesh):
     n = mesh.shape["dp"]
+    to_right = [(k, (k + 1) % n) for k in range(n)]
+    to_left = [(k, (k - 1) % n) for k in range(n)]
 
     def step(x, dy, wg, wu, wd, m_g, m_u, m_d, v_g, v_u, v_d):
         x, dy = x[0], dy[0]
         a0, h1, a1 = forward(x, wg, wu, wd)
-        return backward(a1, dy, h1, a0, wg, wu, wd, (m_g, m_u, m_d, v_g, v_u, v_d), n, "dp")[:9]
+        *made, _, a, b = backward(a1, dy, h1, a0, wg, wu, wd, (m_g, m_u, m_d, v_g, v_u, v_d), n, "dp")
+        with jax.named_scope("first"):
+            la, rb = lax.ppermute(a, "dp", to_right), lax.ppermute(b, "dp", to_left)
+            lb, ra = lax.ppermute(b, "dp", to_right), lax.ppermute(a, "dp", to_left)
+        moments = results(made[3:], a)
+        with jax.named_scope("second"):
+            fa, fb = lax.ppermute(la, "dp", to_right), lax.ppermute(rb, "dp", to_left)
+        weights = results(made[:3], moments[0])
+        new = place_kept((a, b), (la, lb, ra, rb, fa, fb), weights, n, "dp")
+        return (*new, *moments)
 
     seq = P(("rep", "dp"), None, None)
     rows = P(None, "dp", None)

time: 858 us -> 747 us (0.87)
  Pallas kernels: 809 us -> 736 us
  local copies, waits for them, and re-layouts: 47.9 us -> 0.01 us
    pallas_call x1, Pallas kernels: 723 us -> 596 us  [backward(): pl.pallas_call(functools.partial(backward_kernel, n, t // tm, d, ff, axis...]
    pallas_call x0 -> x3, Pallas kernels: none -> 53.9 us  [the longest x2 47.4 us: results(): pl.pallas_call(functools.partial(results_kernel, len(sources), None), in_...]
    unnamed x41 -> x4, local copies, waits for them, and re-layouts: 47.9 us -> 0.01 us
  transfers between devices with their start and end apart: 0 -> 6, of which waited for: 0 -> 1; matrix products, arithmetic and copies ran while one was open for 0% -> 0% of each run, Pallas kernels for 0% -> 6%
where the time goes in v2:
time: 747 us; the launch traced here: 746 us
  Pallas kernels  736 us (99%)
    pallas_call x1, Pallas kernels, backward(): pl.pallas_call(functools.partial(backward_kernel, n, t // tm, d, ff, axis...  596 us
    pallas_call x1, Pallas kernels, forward(): pl.pallas_call(functools.partial(forward_kernel, blocks), grid=(t // tm,)...  85.7 us
    pallas_call x2, Pallas kernels, results(): pl.pallas_call(functools.partial(results_kernel, len(sources), None), in_...  47.4 us
  transfers between devices with their start and end apart: 6, of which 1 were waited for; matrix products, arithmetic and copies ran while one was open for 0% of the time, Pallas kernels for 6%

profile of v2, /device:TPU:112, one launch (start us, length us, event | category | flops | bytes accessed | tf_op | source)
XLA Modules:
  0.0 746.3 jit_solution(5072682472516557129)
XLA Ops:
  0.6 85.7 %forward.1 = (bf16[4096,1024]{1,0:T(8,128)(2,1)}, bf16[4096,1024]{1,0:T(8,128)(2,1)}, bf16[4096,1024]{1,0:T(8,128)(2,1)}) custom-call(bf16[4096,1024]{1,0:T(8,128)(2,1)} %bitcast.2, bf16[2,1024,2816]{2,1,0:T(8,128)(2,1)} %wg_hbm.3, bf16[2,1024,2816]{2,1,0:T(8,128)(2,1)} %wu_hbm.3, bf16[2,2816,1024]{2,1,0:T(8,128)(2,1)} %wd_hbm.3), custom_call_target="tpu_custom_call" | custom-call | flops 70866960384 | bytes 50855936 | tf_op jit(solution)/shard_map/forward/pallas_call | solution.py:73
  86.3 596.1 %backward.1 = (bf16[2,1024,2816]{2,1,0:T(8,128)(2,1)}, bf16[2,1024,2816]{2,1,0:T(8,128)(2,1)}, bf16[2,2816,1024]{2,1,0:T(8,128)(2,1)}, f32[2,256,2816]{2,1,0:T(8...) custom-call(bf16[4096,1024]{1,0:T(8,128)(2,1)} %get-tuple-element.35, ...), custom_call_target="tpu_custom_call" | custom-call | flops 330712481792 | bytes 184549376 | tf_op jit(solution)/shard_map/backward/pallas_call | solution.py:592
  682.5 0.3 collective-permute-start.3
  682.8 1.8 collective-permute-start.1
  684.6 1.4 collective-permute-start.2
  686.0 0.6 collective-permute-start
  686.6 23.4 %results.2 = (f32[2,256,2816]{2,1,0:T(8,128)}, f32[2,256,2816]{2,1,0:T(8,128)}, f32[2,704,1024]{2,1,0:T(8,128)}, f32[2,256,2816]{2,1,0:T(8,128)}, f32[2,256,2816]{2,1,0:T(8,128)}, /*index=5*/f32[2,704,1024]{2,1,0:T(8,128)}) custom-call(f32[2,256,2816]{2,1,0:T(8,128)} %get-tuple-element.43.refs_0_, f32[2,256,2816]{2,1,0:T(8,128)} %get-tuple-element.44.refs_1_, ...), custom_call_target="tpu_custom_call" | custom-call | flops 20000000000 | bytes 69206016 | tf_op jit(solution)/shard_map/results/pallas_call | solution.py:700
  710.0 0.0 collective-permute-done.3.rb
  710.0 2.7 collective-permute-start.5
  712.7 2.2 collective-permute-done.la
  714.9 0.6 collective-permute-start.4
  715.5 0.0 copy-start
  715.5 0.0 copy-start.1
  715.5 24.0 %results.3 = (bf16[2,1024,2816]{2,1,0:T(8,128)(2,1)}, bf16[2,1024,2816]{2,1,0:T(8,128)(2,1)}, bf16[2,2816,1024]{2,1,0:T(8,128)(2,1)}) custom-call(bf16[2,1024,2816]{2,1,0:T(8,128)(2,1)} %get-tuple-element.40.refs_0_, bf16[2,1024,2816]{2,1,0:T(8,128)(2,1)} %get-tuple-element.41.refs_1_, bf16[2,2816,1024]{2,1,0:T(8,128)(2,1)} %get-tuple-element.42.refs_2_, ...), custom_call_target="tpu_custom_call" | custom-call | flops 20000000000 | bytes 69206016 | tf_op jit(solution)/shard_map/results/pallas_call | solution.py:700
  739.5 0.0 collective-permute-done.1.lb
  739.5 0.0 collective-permute-done.2.ra
  739.5 0.0 collective-permute-done.5.fb
  739.5 0.0 collective-permute-done.4.fa
  739.5 0.0 copy-done
  739.6 0.0 copy-done.1
  739.6 6.5 place_kept.1
Async XLA Ops:
  682.5 27.5 %collective-permute-start.3 = (bf16[1664,256]{1,0:T(8,128)(2,1)}, bf16[1664,256]{1,0:T(8,128)(2,1)}, u32[]{:S(2)}, u32[]{:S(2)}) collective-permute-start(bf16[1664,256]{1,0:T(8,128)(2,1)} %get-tuple-element.39.b), channel_id=1, source_target_pairs={{0,3},{1,0},{2,1},{3,2},{4,7},{5,4},{6,5},{7,6},{8,11},{9,8},{10,9... | collective-permute-start | bytes 2555912 | tf_op jit(solution)/shard_map/first/ppermute | solution.py:775
  682.8 56.7 %collective-permute-start.1 = (bf16[1664,256]{1,0:T(8,128)(2,1)}, bf16[1664,256]{1,0:T(8,128)(2,1)}, u32[]{:S(2)}, u32[]{:S(2)}) collective-permute-start(bf16[1664,256]{1,0:T(8,128)(2,1)} %get-tuple-element.39.b), channel_id=1, source_target_pairs={{0,1},{1,2},{2,3},{3,0},{4,5},{5,6},{6,7},{7,4},{8,9},{9,10},{10,1... | collective-permute-start | bytes 2555912 | tf_op jit(solution)/shard_map/first/ppermute | solution.py:776
  684.6 55.0 %collective-permute-start.2 = (bf16[1664,256]{1,0:T(8,128)(2,1)}, bf16[1664,256]{1,0:T(8,128)(2,1)}, u32[]{:S(2)}, u32[]{:S(2)}) collective-permute-start(bf16[1664,256]{1,0:T(8,128)(2,1)} %get-tuple-element.38.refs_6_.a), channel_id=1, source_target_pairs={{0,3},{1,0},{2,1},{3,2},{4,7},{5,4},{6,5},{7,6},{8,11},{9,8},{10,9... | collective-permute-start | bytes 2555912 | tf_op jit(solution)/shard_map/first/ppermute | solution.py:776
  686.0 28.9 %collective-permute-start = (bf16[1664,256]{1,0:T(8,128)(2,1)}, bf16[1664,256]{1,0:T(8,128)(2,1)}, u32[]{:S(2)}, u32[]{:S(2)}) collective-permute-start(bf16[1664,256]{1,0:T(8,128)(2,1)} %get-tuple-element.38.refs_6_.a), channel_id=1, source_target_pairs={{0,1},{1,2},{2,3},{3,0},{4,5},{5,6},{6,7},{7,4},{8,9},{9,10},{10,1... | collective-permute-start | bytes 2555912 | tf_op jit(solution)/shard_map/first/ppermute | solution.py:775
  710.0 29.5 %collective-permute-start.5 = (bf16[1664,256]{1,0:T(8,128)(2,1)}, bf16[1664,256]{1,0:T(8,128)(2,1)}, u32[]{:S(2)}, u32[]{:S(2)}) collective-permute-start(bf16[1664,256]{1,0:T(8,128)(2,1)} %collective-permute-done.3.rb), channel_id=1, source_target_pairs={{0,3},{1,0},{2,1},{3,2},{4,7},{5,4},{6,5},{7,6},{8,11},{9,8},{10,9... | collective-permute-start | bytes 2555912 | tf_op jit(solution)/shard_map/second/ppermute | solution.py:779
  714.9 24.6 %collective-permute-start.4 = (bf16[1664,256]{1,0:T(8,128)(2,1)}, bf16[1664,256]{1,0:T(8,128)(2,1)}, u32[]{:S(2)}, u32[]{:S(2)}) collective-permute-start(bf16[1664,256]{1,0:T(8,128)(2,1)} %collective-permute-done.la), channel_id=1, source_target_pairs={{0,1},{1,2},{2,3},{3,0},{4,5},{5,6},{6,7},{7,4},{8,9},{9,10},{10,1... | collective-permute-start | bytes 2555912 | tf_op jit(solution)/shard_map/second/ppermute | solution.py:779
  715.5 24.0 %copy-start = (bf16[1664,256]{1,0:T(8,128)(2,1)S(1)}, bf16[1664,256]{1,0:T(8,128)(2,1)}, u32[]{:S(2)}) copy-start(bf16[1664,256]{1,0:T(8,128)(2,1)} %get-tuple-element.38.refs_6_.a) | copy-start | bytes 2555908
  715.5 24.0 %copy-start.1 = (bf16[1664,256]{1,0:T(8,128)(2,1)S(1)}, bf16[1664,256]{1,0:T(8,128)(2,1)}, u32[]{:S(2)}) copy-start(bf16[1664,256]{1,0:T(8,128)(2,1)} %get-tuple-element.39.b) | copy-start | bytes 2555908

commit v3 on v2

--- a/solution.py
+++ b/solution.py
@@ -44,24 +44,51 @@
             for c in copies(b):
                 c.start()
 
-    wide = x_ref[...].astype(F32)
-    a0_ref[...] = (wide * norm_scale(wide)).astype(BF16)
+    tm = x_ref.shape[0]
+    halves = (slice(0, tm // 2), slice(tm // 2, tm))
+
+    def hidden(rows, cols):
+        gate = dot(a0_ref[rows, :], wg[:, cols])
+        up = dot(a0_ref[rows, :], wu[:, cols])
+        act[rows, cols] = (gate * jax.nn.sigmoid(gate) * up).astype(BF16)
+
+    def norm(rows):
+        wide = x_ref[rows, :].astype(F32)
+        a0_ref[rows, :] = (wide * norm_scale(wide)).astype(BF16)
+
+    def first():
+        norm(slice(0, tm))
+
+        def block(b, _):
+            for c in copies(b)[:2]:
+                c.wait()
+            hidden(slice(0, tm), pl.ds(pl.multiple_of(b * BLOCK, BLOCK), BLOCK))
+            return 0
+
+        lax.fori_loop(0, blocks, block, 0)
+        for b in range(blocks):
+            copies(b)[2].wait()
+
+    def finish(rows):
+        h = x_ref[rows, :] + dot(act[rows, :], wd[...]).astype(BF16)
+        h_ref[rows, :] = h
+        wide = h.astype(F32)
+        a1_ref[rows, :] = (wide * norm_scale(wide)).astype(BF16)
 
     @pl.when(step == 0)
     def _():
-        for b in range(blocks):
-            for c in copies(b):
-                c.wait()
-
-    for b in range(blocks):
-        cols = slice(b * BLOCK, (b + 1) * BLOCK)
-        gate = dot(a0_ref[...], wg[:, cols])
-        up = dot(a0_ref[...], wu[:, cols])
-        act[:, cols] = (gate * jax.nn.sigmoid(gate) * up).astype(BF16)
-    h = x_ref[...] + dot(act[...], wd[...]).astype(BF16)
-    h_ref[...] = h
-    wide = h.astype(F32)
-    a1_ref[...] = (wide * norm_scale(wide)).astype(BF16)
+        first()
+        for rows in halves:
+            finish(rows)
+
+    @pl.when(step > 0)
+    def _():
+        for rows in halves:
+            norm(rows)
+            for b in range(blocks):
+                hidden(rows, slice(b * BLOCK, (b + 1) * BLOCK))
+        for rows in halves:
+            finish(rows)
 
 
 def forward(x, wg, wu, wd, tm=None):
@@ -96,12 +123,12 @@
     return (w - 0.02 * step).astype(BF16), m, v
 
 
-GU, DOWN, LAST = 0, 1, 2
+GU, DOWN, SMALL = 0, 1, 2
 RING = 6
-LEAD = 4
+LEAD = 3
 QUARTERS = 4
 GROUPS = 3
-KEPT = 11
+KEPT = 12
 SLOTS = 12
 AHEAD = 6
 
@@ -110,11 +137,14 @@
     return jnp.where(it < LEAD, it, 2 * it - LEAD + 1)
 
 
+def pairs_end(blocks):
+    return 4 * blocks - LEAD
+
+
 def pack_kind(p, blocks):
-    paired = (p >= LEAD) & (p < 4 * blocks - LEAD)
-    down = (paired & (lax.rem(p, 2) == 0)) | (p >= 4 * blocks - LEAD)
-    last = down & (lax.rem(pack_down(p, blocks) // QUARTERS, GROUPS) == GROUPS - 1)
-    return {GU: jnp.logical_not(down), DOWN: down & jnp.logical_not(last), LAST: last}
+    down = ((p >= LEAD) & (p < pairs_end(blocks)) & (lax.rem(p + LEAD, 2) == 0)) | (p >= pairs_end(blocks))
+    small = down & (lax.rem(pack_down(p, blocks) // QUARTERS, GROUPS) == 0)
+    return {GU: jnp.logical_not(down), DOWN: down & jnp.logical_not(small), SMALL: small}
 
 
 def pack_block(p):
@@ -122,7 +152,15 @@
 
 
 def pack_down(p, blocks):
-    return jnp.where(p < 4 * blocks - LEAD, jnp.maximum(p - LEAD, 0) // 2, p - 2 * blocks)
+    return jnp.where(p < pairs_end(blocks), jnp.maximum(p - LEAD, 0) // 2, p - 2 * blocks)
+
+
+def block_of(i):
+    j = i - LEAD
+    if isinstance(i, int):
+        return 3 * i + 2 if i < LEAD else 3 * (j % 4) + j // 4
+    j = jnp.maximum(j, 0)
+    return jnp.where(i < LEAD, 3 * i + 2, 3 * lax.rem(j, 4) + j // 4)
 
 
 def backward_kernel(
@@ -151,8 +189,7 @@
     kind_of = functools.partial(pack_kind, blocks=blocks)
 
     def block_cols(it):
-        i = lax.rem(it, blocks)
-        return mult((3 * lax.rem(i, 4) + i // 4) * q, q)
+        return mult(block_of(lax.rem(it, blocks)) * q, q)
 
     def down_group(p):
         return pack_down(p, blocks) // QUARTERS
@@ -161,7 +198,7 @@
         return mult(lax.rem(pack_down(p, blocks), QUARTERS) * q, q)
 
     def height(kind):
-        return {GU: q, DOWN: q // 2, LAST: 3 * UNIT // 2}[kind]
+        return {GU: q, DOWN: q // 2, SMALL: 3 * UNIT // 2}[kind]
 
     def last_row(dev, k):
         u = k // 2
@@ -176,7 +213,7 @@
         lay, cols = 1 - group // GROUPS, pl.ds(down_cols(p), q)
         base = 0 if per_device else dev * (ff // n)
         if kind == DOWN:
-            row = base + lax.rem(group, GROUPS) * 4 * UNIT + dev * UNIT + half * (q // 2)
+            row = base + (lax.rem(group, GROUPS) - 1) * 4 * UNIT + dev * UNIT + half * (q // 2)
             return [(ref_d.at[lay, pl.ds(mult(row, UNIT), q // 2), cols], 0, q // 2)]
         small = UNIT // 2
         return [
@@ -185,12 +222,12 @@
 
     def kept_rows(kind, p):
         k = p - (packs - KEPT)
-        pair, small = q + q // 2, 3 * UNIT // 2
-        row = {
-            GU: k // 2 * pair,
-            DOWN: jnp.where(k < 5, k // 2 * pair + q, 2 * pair + q + (k - 5) * (q // 2)),
-            LAST: 3 * pair + q // 2 + (k - 7) * small,
-        }[kind]
+        small = q // 2
+        pair = q + small
+        if kind == GU:
+            row = k // 2 * pair
+        else:
+            row = jnp.where(k < 8, k // 2 * pair + q, 4 * pair + (k - 8) * small)
         return pl.ds(mult(row, UNIT // 2), height(kind))
 
     def new_pieces(kind, p, dev, half):
@@ -348,10 +385,11 @@
             for c in own_copies(kind, p):
                 c.start()
 
-        @pl.when(jnp.logical_not(leaves(p)))
-        def _():
-            for c in kept_copies(kind, p):
-                c.start()
+        if kind != SMALL:
+            @pl.when(jnp.logical_not(leaves(p)))
+            def _():
+                for c in kept_copies(kind, p):
+                    c.start()
 
     def do_s4(kind, p):
         s = lax.rem(p, RING)
@@ -383,27 +421,26 @@
         for half in range(2):
             pltpu.make_async_copy(wnew.at[s, half, rows], wnew.at[s, half, rows], loc_sem.at[half, s]).wait()
 
-    def each(do, p, among=(GU, DOWN, LAST)):
+    def each(do, p, among=(GU, DOWN, SMALL)):
         for kind, cond in kind_of(p).items():
             if kind in among:
                 @pl.when(cond & (p >= 0) & (p < packs))
                 def _():
                     do(kind, p)
 
-    deep = LEAD + 1
-
-    def lagged(do, p, first, among=(GU, DOWN, LAST)):
-        early = p - first < deep
-        each(do, jnp.where(early, p - first, jnp.where(p - first == deep, -1, p - first - 1)), among)
-
-    def full(p, among=(GU, DOWN, LAST)):
+    deep = 0
+
+    def lagged(do, p, lag):
+        each(do, jnp.where(p < deep, p, jnp.where(p < deep + lag, -1, p - lag)))
+
+    def full(p, among=(GU, DOWN, SMALL)):
         each(do_s1, p, among)
-        lagged(do_s3, p, 1)
+        lagged(do_s3, p - 1, 2)
 
     def half(p):
-        lagged(do_s2, p, 0)
-        lagged(do_s4, p, 2)
-        each(do_s5, p - 5)
+        lagged(do_s2, p, 1)
+        lagged(do_s4, p - 2, 2)
+        each(do_s5, p - 6)
 
 
     def weight_loads(it):
@@ -550,7 +587,7 @@
 
             @pl.when((t == 3) & with_down)
             def _():
-                full(p - 1, (DOWN, LAST))
+                full(p - 1, (DOWN, SMALL))
 
             @pl.when((t == 5) & with_down)
             def _():
@@ -559,7 +596,8 @@
             return 0
 
         lax.fori_loop(0, steps, tile, 0)
-        k, slot = lax.rem(i, 4), lax.rem(i // 4 + jnp.where(layer_1, 0, 1), 2)
+        k = jnp.where(i < LEAD, i, lax.rem(jnp.maximum(i - LEAD, 0), 4))
+        slot = lax.rem(jnp.where(i < LEAD, 0, (i + 1) // 4) + jnp.where(layer_1, 0, GROUPS), 2)
         for c in range(d // q):
             dbuf[slot, pl.ds(mult(k * q, q), q), c * q : (c + 1) * q] = accd[c * q : (c + 1) * q, :].astype(BF16).T
         full(p, (GU,))
@@ -570,12 +608,12 @@
 
     def tail(p, _):
         half(p)
-        full(p + 1, (DOWN, LAST))
+        full(p + 1, (DOWN, SMALL))
         return 0
 
-    lax.fori_loop(4 * blocks - LEAD - 1, end + 5, tail, 0)
+    lax.fori_loop(pairs_end(blocks) - 1, end + 6, tail, 0)
     for p in (end - 2, end - 1):
-        moment_stores_wait(LAST, p)
+        moment_stores_wait(DOWN, p)
 
 
 def backward(a1, dy, h1, a0, wg, wu, wd, moments, n, axis, tm=None):
@@ -639,7 +677,7 @@
 
 
 def kept_height():
-    return 3 * BLOCK + 4 * (BLOCK // 2) + 4 * (3 * UNIT // 2)
+    return 4 * BLOCK + 8 * (BLOCK // 2)
 
 
 def results_kernel(count, rows, *refs):
@@ -709,8 +747,11 @@
     )(*sources, token)
 
 
-def kept_kernel(n, axis, blocks, a, b, la, lb, ra, rb, fa, fb, ng, nu, nd, ng_out, nu_out, nd_out, sem):
+def kept_kernel(n, axis, blocks, away, *refs):
+    halves, (ng_out, nu_out, nd_out, sem) = refs[: 2 * len(away)], refs[2 * len(away) + 3 :]
     q, u = BLOCK, UNIT
+    small = q // 2
+    pair = q + small
     me = lax.axis_index(axis)
     ff = nd_out.shape[1]
     mult = pl.multiple_of
@@ -719,47 +760,38 @@
     def put(src, dst):
         copies.append(pltpu.make_async_copy(src, dst, sem.at[len(copies)]))
 
-    def cols(b):
-        return pl.ds((3 * (b % 4) + b // 4) * q, q)
-
-    for far, halves in enumerate(((a, b), (ra, rb), (fa, fb), (la, lb))):
-        dev = lax.rem(me + far, n)
+    for k, src in enumerate(halves):
+        dev, half = lax.rem(me + away[k // 2], n), k % 2
         base = dev * (ff // n)
-        for half, src in enumerate(halves):
-            out = (ng_out, nu_out)[half]
-            rows = pl.ds(mult(dev * q, q), q)
-            pair = q + q // 2
-            for k in range(3):
-                put(src.at[pl.ds(k * pair, q)], out.at[0, rows, cols(blocks - 3 + k)])
-            for quarter, at_ in enumerate((q, pair + q, 2 * pair + q, 3 * pair)):
-                row = pl.ds(mult(base + 4 * u + dev * u + half * (q // 2), u), q // 2)
-                put(src.at[pl.ds(at_, q // 2)], nd_out.at[0, row, pl.ds(quarter * q, q)])
-            for quarter in range(4):
-                at_ = 3 * pair + q // 2 + quarter * (3 * u // 2)
-                for j in range(3):
-                    piece = 3 * half + j
-                    v = piece // 2
-                    row = base + jnp.where(v < dev, v * u, 8 * u + v * u) + (piece % 2) * (u // 2)
-                    put(src.at[pl.ds(at_ + j * (u // 2), u // 2)], nd_out.at[0, pl.ds(mult(row, u // 2), u // 2), pl.ds(quarter * q, q)])
+        out = (ng_out, nu_out)[half]
+        rows = pl.ds(mult(dev * q, q), q)
+        for b in range(4):
+            put(src.at[pl.ds(b * pair, q)], out.at[0, rows, pl.ds(block_of(blocks - 4 + b) * q, q)])
+        for b in range(8):
+            at_ = b * pair + q if b < 4 else 4 * pair + (b - 4) * small
+            row = pl.ds(mult(base + b // 4 * 4 * u + dev * u + half * small, u), small)
+            put(src.at[pl.ds(at_, small)], nd_out.at[0, row, pl.ds(b % 4 * q, q)])
     for c in copies:
         c.start()
     for c in copies:
         c.wait()
 
 
-def place_kept(own, parts, weights, n, axis):
+def place_kept(parts, away, weights, n, axis):
     blocks = weights[0].shape[-1] // BLOCK
     vmem = pl.BlockSpec(memory_space=pltpu.VMEM)
+    count = len(parts)
     return pl.pallas_call(
-        functools.partial(kept_kernel, n, axis, blocks),
-        in_specs=[vmem] * 8 + [ANY] * 3,
+        functools.partial(kept_kernel, n, axis, blocks, away),
+        in_specs=[vmem] * count + [ANY] * 3,
         out_specs=[ANY] * 3,
         out_shape=[jax.ShapeDtypeStruct(w.shape, w.dtype) for w in weights],
-        input_output_aliases={8: 0, 9: 1, 10: 2},
-        scratch_shapes=[pltpu.SemaphoreType.DMA((8 * (3 + 4 + 12),))],
-        compiler_params=pltpu.CompilerParams(vmem_limit_bytes=40 * MIB),
+        input_output_aliases={count + k: k for k in range(3)},
+        scratch_shapes=[pltpu.SemaphoreType.DMA((count * 12,))],
+        compiler_params=pltpu.CompilerParams(vmem_limit_bytes=62 * MIB),
+        cost_estimate=pl.CostEstimate(flops=10**9, bytes_accessed=count * 4 * MIB, transcendentals=0),
         name="place_kept",
-    )(*own, *parts, *weights)
+    )(*parts, *weights)
 
 
 def solution(mesh):
@@ -770,16 +802,18 @@
     def step(x, dy, wg, wu, wd, m_g, m_u, m_d, v_g, v_u, v_d):
         x, dy = x[0], dy[0]
         a0, h1, a1 = forward(x, wg, wu, wd)
-        *made, _, a, b = backward(a1, dy, h1, a0, wg, wu, wd, (m_g, m_u, m_d, v_g, v_u, v_d), n, "dp")
-        with jax.named_scope("first"):
-            la, rb = lax.ppermute(a, "dp", to_right), lax.ppermute(b, "dp", to_left)
-            lb, ra = lax.ppermute(b, "dp", to_right), lax.ppermute(a, "dp", to_left)
-        moments = results(made[3:], a)
-        with jax.named_scope("second"):
-            fa, fb = lax.ppermute(la, "dp", to_right), lax.ppermute(rb, "dp", to_left)
-        weights = results(made[:3], moments[0])
-        new = place_kept((a, b), (la, lb, ra, rb, fa, fb), weights, n, "dp")
-        return (*new, *moments)
+        ng, nu, nd, mg, mu, md, vg, vu, vd, _, a, b = backward(a1, dy, h1, a0, wg, wu, wd, (m_g, m_u, m_d, v_g, v_u, v_d), n, "dp")
+        la, rb = lax.ppermute(a, "dp", to_right), lax.ppermute(b, "dp", to_left)
+        mg, mu, vg, vu = results((mg, mu, vg, vu), a)
+        a, b, mg = lax.optimization_barrier((a, b, mg))
+        lb, ra = lax.ppermute(b, "dp", to_right), lax.ppermute(a, "dp", to_left)
+        md, vd, nd = results((md, vd, nd), mg)
+        la, rb, md = lax.optimization_barrier((la, rb, md))
+        fa, fb = lax.ppermute(la, "dp", to_right), lax.ppermute(rb, "dp", to_left)
+        ng, nu = results((ng, nu), md)
+        new = place_kept((a, b, ra, rb, la, lb), (0, 1, n - 1), (ng, nu, nd), n, "dp")
+        new = place_kept((fa, fb), (2,), new, n, "dp")
+        return (*new, mg, mu, md, vg, vu, vd)
 
     seq = P(("rep", "dp"), None, None)
     rows = P(None, "dp", None)

time: 747 us -> 709 us (0.949)
  Pallas kernels: 736 us -> 697 us
    pallas_call x1, Pallas kernels: 596 us -> 556 us  [backward(): pl.pallas_call(functools.partial(backward_kernel, n, t // tm, d, ff, axis...]
    pallas_call x2 -> x3, Pallas kernels: 47.4 us -> 49.5 us  [results(): pl.pallas_call(functools.partial(results_kernel, len(sources), None), in_...]
  transfers between devices with their start and end apart: 6 -> 6, of which waited for: 1 -> 2; matrix products, arithmetic and copies ran while one was open for 0% -> 0% of each run, Pallas kernels for 6% -> 8%
where the time goes in v3:
time: 709 us
  Pallas kernels  697 us (98%)
  starting transfers between devices  8.73 us (1%)
    pallas_call x1, Pallas kernels, backward(): pl.pallas_call(functools.partial(backward_kernel, n, t // tm, d, ff, axis...  556 us
    pallas_call x1, Pallas kernels, forward(): pl.pallas_call(functools.partial(forward_kernel, blocks), grid=(t // tm,)...  81.4 us
    pallas_call x3, Pallas kernels, results(): pl.pallas_call(functools.partial(results_kernel, len(sources), None), in_...  49.5 us
  transfers between devices with their start and end apart: 6, of which 2 were waited for; matrix products, arithmetic and copies ran while one was open for 0% of the time, Pallas kernels for 8%

profile of v3, /device:TPU:112, one launch (start us, length us, event | category | flops | bytes accessed | tf_op | source)
XLA Modules:
  0.0 708.7 jit_solution(13264185315272930574)
XLA Ops:
  0.6 81.4 %forward.1 = (bf16[4096,1024]{1,0:T(8,128)(2,1)}, bf16[4096,1024]{1,0:T(8,128)(2,1)}, bf16[4096,1024]{1,0:T(8,128)(2,1)}) custom-call(bf16[4096,1024]{1,0:T(8,128)(2,1)} %bitcast.2, bf16[2,1024,2816]{2,1,0:T(8,128)(2,1)} %wg_hbm.3, bf16[2,1024,2816]{2,1,0:T(8,128)(2,1)} %wu_hbm.3, bf16[2,2816,1024]{2,1,0:T(8,128)(2,1)} %wd_hbm.3), custom_call_target="tpu_custom_call" | custom-call | flops 70866960384 | bytes 50855936 | tf_op jit(solution)/shard_map/forward/pallas_call | solution.py:100
  82.1 556.4 %backward.1 = (bf16[2,1024,2816]{2,1,0:T(8,128)(2,1)}, bf16[2,1024,2816]{2,1,0:T(8,128)(2,1)}, bf16[2,2816,1024]{2,1,0:T(8,128)(2,1)}, f32[2,256,2816]{2,1,0:T(8...) custom-call(bf16[4096,1024]{1,0:T(8,128)(2,1)} %get-tuple-element.44, ...), custom_call_target="tpu_custom_call" | custom-call | flops 330712481792 | bytes 184549376 | tf_op jit(solution)/shard_map/backward/pallas_call | solution.py:630
  638.5 1.3 collective-permute-start
  639.7 2.0 collective-permute-start.1
  641.8 0.0 copy-start
  641.8 16.5 %results.3 = (f32[2,256,2816]{2,1,0:T(8,128)}, f32[2,256,2816]{2,1,0:T(8,128)}, f32[2,256,2816]{2,1,0:T(8,128)}, f32[2,256,2816]{2,1,0:T(8,128)}) custom-call(f32[2,256,2816]{2,1,0:T(8,128)} %get-tuple-element.52.refs_0_, f32[2,256,2816]{2,1,0:T(8,128)} %get-tuple-element.53.refs_1_, f32[2,256,2816]{2,1,0:T(8,128)} %get-tuple-element.54.refs_2_, ...), custom_call_target="tpu_custom_call" | custom-call | flops 20000000000 | bytes 46137344 | tf_op jit(solution)/shard_map/results/pallas_call | solution.py:738
  658.3 0.0 copy-done
  658.3 1.3 collective-permute-start.4
  659.6 0.8 collective-permute-start.5
  660.4 16.6 %results.4 = (f32[2,704,1024]{2,1,0:T(8,128)}, f32[2,704,1024]{2,1,0:T(8,128)}, bf16[2,2816,1024]{2,1,0:T(8,128)(2,1)}) custom-call(f32[2,704,1024]{2,1,0:T(8,128)} %get-tuple-element.49.refs_0_, f32[2,704,1024]{2,1,0:T(8,128)} %get-tuple-element.50.refs_1_, bf16[2,2816,1024]{2,1,0:T(8,128)(2,1)} %get-tuple-element.51.refs_2_, ...), custom_call_target="tpu_custom_call" | custom-call | flops 20000000000 | bytes 46137344 | tf_op jit(solution)/shard_map/results/pallas_call | solution.py:738
  677.0 0.0 collective-permute-done.refs_4_
  677.0 0.0 collective-permute-done.1.refs_3_
  677.1 0.1 collective-permute-start.2
  677.2 3.2 collective-permute-start.3
  680.4 16.4 %results.5 = (bf16[2,1024,2816]{2,1,0:T(8,128)(2,1)}, bf16[2,1024,2816]{2,1,0:T(8,128)(2,1)}) custom-call(bf16[2,1024,2816]{2,1,0:T(8,128)(2,1)} %get-tuple-element.63.refs_0_, bf16[2,1024,2816]{2,1,0:T(8,128)(2,1)} %get-tuple-element.64.refs_1_, f32[2,704,1024]{2,1,0:T(8,128)} %get-tuple-element.40.refs_2_), custom_call_target="tpu_custom_call" | custom-call | flops 20000000000 | bytes 46137344 | tf_op jit(solution)/shard_map/results/pallas_call | solution.py:738
  696.8 0.0 collective-permute-done.4.refs_2_
  696.8 0.0 collective-permute-done.5.refs_5_
  696.8 6.1 place_kept.2
  702.9 2.4 collective-permute-done.2.refs_0_
  705.4 0.1 collective-permute-done.3.refs_1_
  705.5 3.0 place_kept.3
Async XLA Ops:
  638.5 38.6 %collective-permute-start = (bf16[2048,256]{1,0:T(8,128)(2,1)}, bf16[2048,256]{1,0:T(8,128)(2,1)}, u32[]{:S(2)}, u32[]{:S(2)}) collective-permute-start(bf16[2048,256]{1,0:T(8,128)(2,1)} %get-tuple-element.61.refs_4_.refs_0_), channel_id=1, source_target_pairs={{0,1},{1,2},{2,3},{3,0},{4,5},{5,6},{6,7},{7,4},{8,9},{9,10},{10,1... | collective-permute-start | bytes 3145736 | tf_op jit(solution)/shard_map/ppermute | solution.py:806
  639.7 37.3 %collective-permute-start.1 = (bf16[2048,256]{1,0:T(8,128)(2,1)}, bf16[2048,256]{1,0:T(8,128)(2,1)}, u32[]{:S(2)}, u32[]{:S(2)}) collective-permute-start(bf16[2048,256]{1,0:T(8,128)(2,1)} %get-tuple-element.62.refs_1_), channel_id=1, source_target_pairs={{0,3},{1,0},{2,1},{3,2},{4,7},{5,4},{6,5},{7,6},{8,11},{9,8},{10,9... | collective-permute-start | bytes 3145736 | tf_op jit(solution)/shard_map/ppermute | solution.py:806
  641.8 16.5 %copy-start = (bf16[2048,256]{1,0:T(8,128)(2,1)S(1)}, bf16[2048,256]{1,0:T(8,128)(2,1)}, u32[]{:S(2)}) copy-start(bf16[2048,256]{1,0:T(8,128)(2,1)} %get-tuple-element.61.refs_4_.refs_0_) | copy-start | bytes 3145732
  658.3 38.5 %collective-permute-start.4 = (bf16[2048,256]{1,0:T(8,128)(2,1)S(1)}, bf16[2048,256]{1,0:T(8,128)(2,1)}, u32[]{:S(2)}, u32[]{:S(2)}) collective-permute-start(bf16[2048,256]{1,0:T(8,128)(2,1)S(1)} %copy-done), channel_id=1, source_target_pairs={{0,3},{1,0},{2,1},{3,2},{4,7},{5,4},{6,5},{7,6},{8,11},{9,8},{10,9... | collective-permute-start | bytes 3145736 | tf_op jit(solution)/shard_map/ppermute | solution.py:809
  659.6 37.2 %collective-permute-start.5 = (bf16[2048,256]{1,0:T(8,128)(2,1)}, bf16[2048,256]{1,0:T(8,128)(2,1)}, u32[]{:S(2)}, u32[]{:S(2)}) collective-permute-start(bf16[2048,256]{1,0:T(8,128)(2,1)} %get-tuple-element.62.refs_1_), channel_id=1, source_target_pairs={{0,1},{1,2},{2,3},{3,0},{4,5},{5,6},{6,7},{7,4},{8,9},{9,10},{10,1... | collective-permute-start | bytes 3145736 | tf_op jit(solution)/shard_map/ppermute | solution.py:809
  677.1 28.3 %collective-permute-start.2 = (bf16[2048,256]{1,0:T(8,128)(2,1)}, bf16[2048,256]{1,0:T(8,128)(2,1)}, u32[]{:S(2)}, u32[]{:S(2)}) collective-permute-start(bf16[2048,256]{1,0:T(8,128)(2,1)} %collective-permute-done.refs_4_), channel_id=1, source_target_pairs={{0,1},{1,2},{2,3},{3,0},{4,5},{5,6},{6,7},{7,4},{8,9},{9,10},{10,1... | collective-permute-start | bytes 3145736 | tf_op jit(solution)/shard_map/ppermute | solution.py:812
  677.2 28.3 %collective-permute-start.3 = (bf16[2048,256]{1,0:T(8,128)(2,1)}, bf16[2048,256]{1,0:T(8,128)(2,1)}, u32[]{:S(2)}, u32[]{:S(2)}) collective-permute-start(bf16[2048,256]{1,0:T(8,128)(2,1)} %collective-permute-done.1.refs_3_), channel_id=1, source_target_pairs={{0,3},{1,0},{2,1},{3,2},{4,7},{5,4},{6,5},{7,6},{8,11},{9,8},{10,9... | collective-permute-start | bytes 3145736 | tf_op jit(solution)/shard_map/ppermute | solution.py:812

commit v4 on v3

--- a/solution.py
+++ b/solution.py
@@ -12,6 +12,7 @@
 UNIT = 64
 MIB = 2**20
 TM = 512
+TB = 1024
 ANY = pl.BlockSpec(memory_space=pl.ANY)
 
 
@@ -125,6 +126,8 @@
 
 GU, DOWN, SMALL = 0, 1, 2
 RING = 6
+KEEP_RING = 3
+OWN_RING = 4
 LEAD = 3
 QUARTERS = 4
 GROUPS = 3
@@ -167,7 +170,7 @@
     n, steps, d, ff, axis,
     a1_hbm, dy_hbm, h1_hbm, a0_hbm, wg_hbm, wu_hbm, wd_hbm, mg_hbm, mu_hbm, md_hbm, vg_hbm, vu_hbm, vd_hbm,
     ng_hbm, nu_hbm, nd_hbm, mg_out, mu_out, md_out, vg_out, vu_out, vd_out, dh_hbm, kept_a, kept_b,
-    tiles, at, dht, wgu, wdn, wdt, wgut, accgu, accd, da, dbuf, hout,
+    tiles, at, dht, wgu, wdn, wdt, wgut, accgu, accd, da, dbuf,
     send, keep, own, r1, r2, s2, wnew, mvin, win, mvout,
     tile_sem, weight_sem, hout_sem, s1s, s1r, s2s, s2r, g1s, g1r, g2s, g2r, loc_sem, mvin_sem, mvout_sem,
 ):
@@ -331,10 +334,11 @@
         send[s, 0, h : 2 * h, :] = part(right, 1)
         send[s, 1, :h, :] = part(far, 1)
         send[s, 1, h : 2 * h, :] = part(left, 0)
-        keep[s, 0, :h, :] = part(right, 0)
-        keep[s, 1, :h, :] = part(left, 1)
-        own[s, 0, :h, :] = part(me, 0)
-        own[s, 1, :h, :] = part(me, 1)
+        sk, so = lax.rem(p, KEEP_RING), lax.rem(p, OWN_RING)
+        keep[sk, 0, :h, :] = part(right, 0)
+        keep[sk, 1, :h, :] = part(left, 1)
+        own[so, 0, :h, :] = part(me, 0)
+        own[so, 1, :h, :] = part(me, 1)
 
     def do_s1(kind, p):
         stage(kind, p)
@@ -347,7 +351,7 @@
             c.start()
         for way in range(2):
             s1_copy(kind, p, way).wait_recv()
-            s2[s, way, :h, :] = (keep[s, way, :h, :].astype(F32) + r1[s, way, :h, :].astype(F32)).astype(BF16)
+            s2[s, way, :h, :] = (keep[lax.rem(p, KEEP_RING), way, :h, :].astype(F32) + r1[s, way, :h, :].astype(F32)).astype(BF16)
             s2_copy(kind, p, way).start()
 
     def do_s3(kind, p):
@@ -364,7 +368,7 @@
             rows = pl.ds(mult(u * (UNIT // 2), UNIT // 2), UNIT // 2)
             rest = pl.ds(mult(h + u * (UNIT // 2), UNIT // 2), UNIT // 2)
             for half in range(2):
-                g = own[s, half, rows, :].astype(F32) + r1[s, 1 - half, rest, :].astype(F32) + r2[s, half, rows, :].astype(F32)
+                g = own[lax.rem(p, OWN_RING), half, rows, :].astype(F32) + r1[s, 1 - half, rest, :].astype(F32) + r2[s, half, rows, :].astype(F32)
                 g = g.astype(BF16).astype(F32)
                 w, m, v = adamw(win[b, half, rows, :].astype(F32), mvin[b, 2 * half, rows, :], mvin[b, 2 * half + 1, rows, :], g)
                 wnew[s, half, rows, :] = w
@@ -428,7 +432,7 @@
                 def _():
                     do(kind, p)
 
-    deep = 0
+    deep = 2
 
     def lagged(do, p, lag):
         each(do, jnp.where(p < deep, p, jnp.where(p < deep + lag, -1, p - lag)))
@@ -493,40 +497,53 @@
             for r in (slice(0, d // 2), slice(d // 2, d)):
                 accd[r, :] += dot(dht[r, rows], act)
 
+    part_rows = min(tm, 256)
+    quarter = steps // 4
+
     def between_layers():
         def loads(t):
             return tile_loads(h1_hbm, dy_hbm, t)
 
         def store(t):
-            return pltpu.make_async_copy(hout.at[lax.rem(t, 2)], dh_hbm.at[pl.ds(mult(t * tm, tm), tm), :], hout_sem.at[lax.rem(t, 2)])
+            b = lax.rem(t, 2)
+            return pltpu.make_async_copy(tiles.at[b, 1], dh_hbm.at[pl.ds(mult(t * tm, tm), tm), :], hout_sem.at[b])
 
         for c in loads(0):
             c.start()
 
         def tile(t, _):
+            b = lax.rem(t, 2)
+            for c in loads(t):
+                c.wait()
+
+            @pl.when(t >= 1)
+            def _():
+                store(t - 1).wait()
+
             @pl.when(t + 1 < steps)
             def _():
                 for c in loads(t + 1):
                     c.start()
 
-            for c in loads(t):
-                c.wait()
-
-            @pl.when(t >= 2)
-            def _():
-                store(t - 2).wait()
-
-            b = lax.rem(t, 2)
-            g = da[pl.ds(mult(t * tm, tm), tm), :].astype(BF16).astype(F32)
-            wide = tiles[b, 0].astype(F32)
-            scale = norm_scale(wide)
-            inner = jnp.mean(g * wide, -1, keepdims=True)
-            hout[b] = tiles[b, 1] + (scale * g - wide * (scale * scale * scale * inner)).astype(BF16)
+            def part(k, _):
+                rows = pl.ds(mult(k * part_rows, part_rows), part_rows)
+                g = da[pl.ds(mult(t * tm + k * part_rows, part_rows), part_rows), :].astype(BF16).astype(F32)
+                wide = tiles[b, 0, rows, :].astype(F32)
+                scale = norm_scale(wide)
+                inner = jnp.mean(g * wide, -1, keepdims=True)
+                tiles[b, 1, rows, :] = tiles[b, 1, rows, :] + (scale * g - wide * (scale * scale * scale * inner)).astype(BF16)
+                return 0
+
+            lax.fori_loop(0, tm // part_rows, part, 0)
             store(t).start()
+
+            @pl.when(t == steps // 2 - 1)
+            def _():
+                half(pack_of_block(blocks - 1))
+
             return 0
 
         lax.fori_loop(0, steps, tile, 0)
-        store(steps - 2).wait()
         store(steps - 1).wait()
 
     for c in weight_loads(0):
@@ -581,15 +598,15 @@
             def _():
                 compute(b, wb, t, False)
 
-            @pl.when((t == 1) & (it >= 1))
+            @pl.when((t == quarter - 1) & (it >= 1) & (it != blocks))
             def _():
                 half(pack_of_block(it - 1))
 
-            @pl.when((t == 3) & with_down)
+            @pl.when((t == 2 * quarter - 1) & with_down)
             def _():
                 full(p - 1, (DOWN, SMALL))
 
-            @pl.when((t == 5) & with_down)
+            @pl.when((t == 3 * quarter - 1) & with_down)
             def _():
                 half(p - 1)
 
@@ -617,7 +634,7 @@
 
 
 def backward(a1, dy, h1, a0, wg, wu, wd, moments, n, axis, tm=None):
-    tm = tm or TM
+    tm = tm or TB
     t, d = dy.shape
     ff = wg.shape[-1]
     q = BLOCK
@@ -644,10 +661,9 @@
             V((d, q), F32),
             V((t, d), F32),
             V((2, 4 * q, d), BF16),
-            V((2, tm, d), BF16),
             V((RING, 2, 2 * q, q), BF16),
-            V((RING, 2, q, q), BF16),
-            V((RING, 2, q, q), BF16),
+            V((KEEP_RING, 2, q, q), BF16),
+            V((OWN_RING, 2, q, q), BF16),
             V((RING, 2, 2 * q, q), BF16),
             V((RING, 2, q, q), BF16),
             V((RING, 2, q, q), BF16),
@@ -670,7 +686,7 @@
             DMA((2, 6)),
             DMA((2, 4)),
         ],
-        compiler_params=pltpu.CompilerParams(vmem_limit_bytes=62 * MIB, collective_id=0, has_side_effects=True),
+        compiler_params=pltpu.CompilerParams(vmem_limit_bytes=67_043_328, collective_id=0, has_side_effects=True),
         cost_estimate=pl.CostEstimate(flops=28 * t * d * ff, bytes_accessed=44 * t * d, transcendentals=2 * t * ff),
         name="backward",
     )(a1, dy, h1, a0, wg, wu, wd, *moments)

time: 709 us -> 700 us (0.987)
  Pallas kernels: 697 us -> 689 us
    pallas_call x1, Pallas kernels: 556 us -> 549 us  [backward(): pl.pallas_call(functools.partial(backward_kernel, n, t // tm, d, ff, axis...]
  transfers between devices with their start and end apart: 6 -> 6, of which waited for: 2 -> 1; matrix products, arithmetic and copies ran while one was open for 0% -> 0% of each run, Pallas kernels for 8% -> 8%
where the time goes in v4:
time: 700 us
  Pallas kernels  689 us (98%)
  starting transfers between devices  8.73 us (1%)
    pallas_call x1, Pallas kernels, backward(): pl.pallas_call(functools.partial(backward_kernel, n, t // tm, d, ff, axis...  549 us
    pallas_call x1, Pallas kernels, forward(): pl.pallas_call(functools.partial(forward_kernel, blocks), grid=(t // tm,)...  81.4 us
    pallas_call x3, Pallas kernels, results(): pl.pallas_call(functools.partial(results_kernel, len(sources), None), in_...  49.5 us
  transfers between devices with their start and end apart: 6, of which 1 were waited for; matrix products, arithmetic and copies ran while one was open for 0% of the time, Pallas kernels for 8%

profile of v4, /device:TPU:112, one launch (start us, length us, event | category | flops | bytes accessed | tf_op | source)
XLA Modules:
  0.0 700.0 jit_solution(2482644588918964483)
XLA Ops:
  0.6 81.4 %forward.1 = (bf16[4096,1024]{1,0:T(8,128)(2,1)}, bf16[4096,1024]{1,0:T(8,128)(2,1)}, bf16[4096,1024]{1,0:T(8,128)(2,1)}) custom-call(bf16[4096,1024]{1,0:T(8,128)(2,1)} %bitcast.2, bf16[2,1024,2816]{2,1,0:T(8,128)(2,1)} %wg_hbm.3, bf16[2,1024,2816]{2,1,0:T(8,128)(2,1)} %wu_hbm.3, bf16[2,2816,1024]{2,1,0:T(8,128)(2,1)} %wd_hbm.3), custom_call_target="tpu_custom_call" | custom-call | flops 70866960384 | bytes 50855936 | tf_op jit(solution)/shard_map/forward/pallas_call | solution.py:101
  82.1 549.0 %backward.1 = (bf16[2,1024,2816]{2,1,0:T(8,128)(2,1)}, bf16[2,1024,2816]{2,1,0:T(8,128)(2,1)}, bf16[2,2816,1024]{2,1,0:T(8,128)(2,1)}, f32[2,256,2816]{2,1,0:T(8...) custom-call(bf16[4096,1024]{1,0:T(8,128)(2,1)} %get-tuple-element.44, ...), custom_call_target="tpu_custom_call" | custom-call | flops 330712481792 | bytes 184549376 | tf_op jit(solution)/shard_map/backward/pallas_call | solution.py:647
  631.0 1.3 collective-permute-start
  632.3 2.0 collective-permute-start.1
  634.4 0.0 copy-start
  634.4 16.5 %results.3 = (f32[2,256,2816]{2,1,0:T(8,128)}, f32[2,256,2816]{2,1,0:T(8,128)}, f32[2,256,2816]{2,1,0:T(8,128)}, f32[2,256,2816]{2,1,0:T(8,128)}) custom-call(f32[2,256,2816]{2,1,0:T(8,128)} %get-tuple-element.52.refs_0_, f32[2,256,2816]{2,1,0:T(8,128)} %get-tuple-element.53.refs_1_, f32[2,256,2816]{2,1,0:T(8,128)} %get-tuple-element.54.refs_2_, ...), custom_call_target="tpu_custom_call" | custom-call | flops 20000000000 | bytes 46137344 | tf_op jit(solution)/shard_map/results/pallas_call | solution.py:754
  650.9 0.0 copy-done
  650.9 1.3 collective-permute-start.4
  652.2 0.8 collective-permute-start.5
  653.0 16.6 %results.4 = (f32[2,704,1024]{2,1,0:T(8,128)}, f32[2,704,1024]{2,1,0:T(8,128)}, bf16[2,2816,1024]{2,1,0:T(8,128)(2,1)}) custom-call(f32[2,704,1024]{2,1,0:T(8,128)} %get-tuple-element.49.refs_0_, f32[2,704,1024]{2,1,0:T(8,128)} %get-tuple-element.50.refs_1_, bf16[2,2816,1024]{2,1,0:T(8,128)(2,1)} %get-tuple-element.51.refs_2_, ...), custom_call_target="tpu_custom_call" | custom-call | flops 20000000000 | bytes 46137344 | tf_op jit(solution)/shard_map/results/pallas_call | solution.py:754
  669.6 0.0 collective-permute-done.refs_4_
  669.6 0.0 collective-permute-done.1.refs_3_
  669.6 0.1 collective-permute-start.2
  669.7 3.2 collective-permute-start.3
  672.9 16.4 %results.5 = (bf16[2,1024,2816]{2,1,0:T(8,128)(2,1)}, bf16[2,1024,2816]{2,1,0:T(8,128)(2,1)}) custom-call(bf16[2,1024,2816]{2,1,0:T(8,128)(2,1)} %get-tuple-element.63.refs_0_, bf16[2,1024,2816]{2,1,0:T(8,128)(2,1)} %get-tuple-element.64.refs_1_, f32[2,704,1024]{2,1,0:T(8,128)} %get-tuple-element.40.refs_2_), custom_call_target="tpu_custom_call" | custom-call | flops 20000000000 | bytes 46137344 | tf_op jit(solution)/shard_map/results/pallas_call | solution.py:754
  689.4 0.0 collective-permute-done.4.refs_2_
  689.4 0.0 collective-permute-done.5.refs_5_
  689.4 6.1 place_kept.2
  695.5 1.3 collective-permute-done.2.refs_0_
  696.8 0.0 collective-permute-done.3.refs_1_
  696.8 3.0 place_kept.3
Async XLA Ops:
  631.0 38.6 %collective-permute-start = (bf16[2048,256]{1,0:T(8,128)(2,1)}, bf16[2048,256]{1,0:T(8,128)(2,1)}, u32[]{:S(2)}, u32[]{:S(2)}) collective-permute-start(bf16[2048,256]{1,0:T(8,128)(2,1)} %get-tuple-element.61.refs_4_.refs_0_), channel_id=1, source_target_pairs={{0,1},{1,2},{2,3},{3,0},{4,5},{5,6},{6,7},{7,4},{8,9},{9,10},{10,1... | collective-permute-start | bytes 3145736 | tf_op jit(solution)/shard_map/ppermute | solution.py:822
  632.3 37.3 %collective-permute-start.1 = (bf16[2048,256]{1,0:T(8,128)(2,1)}, bf16[2048,256]{1,0:T(8,128)(2,1)}, u32[]{:S(2)}, u32[]{:S(2)}) collective-permute-start(bf16[2048,256]{1,0:T(8,128)(2,1)} %get-tuple-element.62.refs_1_), channel_id=1, source_target_pairs={{0,3},{1,0},{2,1},{3,2},{4,7},{5,4},{6,5},{7,6},{8,11},{9,8},{10,9... | collective-permute-start | bytes 3145736 | tf_op jit(solution)/shard_map/ppermute | solution.py:822
  634.4 16.5 %copy-start = (bf16[2048,256]{1,0:T(8,128)(2,1)S(1)}, bf16[2048,256]{1,0:T(8,128)(2,1)}, u32[]{:S(2)}) copy-start(bf16[2048,256]{1,0:T(8,128)(2,1)} %get-tuple-element.61.refs_4_.refs_0_) | copy-start | bytes 3145732
  650.9 38.5 %collective-permute-start.4 = (bf16[2048,256]{1,0:T(8,128)(2,1)S(1)}, bf16[2048,256]{1,0:T(8,128)(2,1)}, u32[]{:S(2)}, u32[]{:S(2)}) collective-permute-start(bf16[2048,256]{1,0:T(8,128)(2,1)S(1)} %copy-done), channel_id=1, source_target_pairs={{0,3},{1,0},{2,1},{3,2},{4,7},{5,4},{6,5},{7,6},{8,11},{9,8},{10,9... | collective-permute-start | bytes 3145736 | tf_op jit(solution)/shard_map/ppermute | solution.py:825
  652.2 37.2 %collective-permute-start.5 = (bf16[2048,256]{1,0:T(8,128)(2,1)}, bf16[2048,256]{1,0:T(8,128)(2,1)}, u32[]{:S(2)}, u32[]{:S(2)}) collective-permute-start(bf16[2048,256]{1,0:T(8,128)(2,1)} %get-tuple-element.62.refs_1_), channel_id=1, source_target_pairs={{0,1},{1,2},{2,3},{3,0},{4,5},{5,6},{6,7},{7,4},{8,9},{9,10},{10,1... | collective-permute-start | bytes 3145736 | tf_op jit(solution)/shard_map/ppermute | solution.py:825
  669.6 27.2 %collective-permute-start.2 = (bf16[2048,256]{1,0:T(8,128)(2,1)}, bf16[2048,256]{1,0:T(8,128)(2,1)}, u32[]{:S(2)}, u32[]{:S(2)}) collective-permute-start(bf16[2048,256]{1,0:T(8,128)(2,1)} %collective-permute-done.refs_4_), channel_id=1, source_target_pairs={{0,1},{1,2},{2,3},{3,0},{4,5},{5,6},{6,7},{7,4},{8,9},{9,10},{10,1... | collective-permute-start | bytes 3145736 | tf_op jit(solution)/shard_map/ppermute | solution.py:828
  669.7 27.0 %collective-permute-start.3 = (bf16[2048,256]{1,0:T(8,128)(2,1)}, bf16[2048,256]{1,0:T(8,128)(2,1)}, u32[]{:S(2)}, u32[]{:S(2)}) collective-permute-start(bf16[2048,256]{1,0:T(8,128)(2,1)} %collective-permute-done.1.refs_3_), channel_id=1, source_target_pairs={{0,3},{1,0},{2,1},{3,2},{4,7},{5,4},{6,5},{7,6},{8,11},{9,8},{10,9... | collective-permute-start | bytes 3145736 | tf_op jit(solution)/shard_map/ppermute | solution.py:828

commit v5 on v4

--- a/solution.py
+++ b/solution.py
@@ -356,6 +356,7 @@
 
     def do_s3(kind, p):
         s, b, h = lax.rem(p, RING), lax.rem(p, 2), height(kind)
+        grain = h if kind == SMALL else UNIT * 2
         moment_loads_wait(kind, p)
         for k, cond in kind_of(p - 2).items():
             @pl.when(cond & (p >= 2))
@@ -365,8 +366,8 @@
             s2_copy(kind, p, way).wait_recv()
 
         def rows_of(u, _):
-            rows = pl.ds(mult(u * (UNIT // 2), UNIT // 2), UNIT // 2)
-            rest = pl.ds(mult(h + u * (UNIT // 2), UNIT // 2), UNIT // 2)
+            rows = pl.ds(mult(u * grain, grain), grain)
+            rest = pl.ds(mult(h + u * grain, UNIT // 2), grain)
             for half in range(2):
                 g = own[lax.rem(p, OWN_RING), half, rows, :].astype(F32) + r1[s, 1 - half, rest, :].astype(F32) + r2[s, half, rows, :].astype(F32)
                 g = g.astype(BF16).astype(F32)
@@ -376,7 +377,7 @@
                 mvout[b, 2 * half + 1, rows, :] = v
             return 0
 
-        lax.fori_loop(0, h // (UNIT // 2), rows_of, 0)
+        lax.fori_loop(0, h // grain, rows_of, 0)
         for c in moment_stores(kind, p):
             c.start()
 

time: 700 us -> 700 us (level)
  no operation moved by 1% of the time
where the time goes in v5:
time: 700 us; the launch traced here: 699 us
  Pallas kernels  688 us (98%)
  starting transfers between devices  8.73 us (1%)
    pallas_call x1, Pallas kernels, backward(): pl.pallas_call(functools.partial(backward_kernel, n, t // tm, d, ff, axis...  548 us
    pallas_call x1, Pallas kernels, forward(): pl.pallas_call(functools.partial(forward_kernel, blocks), grid=(t // tm,)...  81.4 us
    pallas_call x3, Pallas kernels, results(): pl.pallas_call(functools.partial(results_kernel, len(sources), None), in_...  49.5 us
  transfers between devices with their start and end apart: 6, of which 1 were waited for; matrix products, arithmetic and copies ran while one was open for 0% of the time, Pallas kernels for 8%

profile of v5, /device:TPU:112, one launch (start us, length us, event | category | flops | bytes accessed | tf_op | source)
XLA Modules:
  0.0 699.3 jit_solution(377327372953002758)
XLA Ops:
  0.6 81.4 %forward.1 = (bf16[4096,1024]{1,0:T(8,128)(2,1)}, bf16[4096,1024]{1,0:T(8,128)(2,1)}, bf16[4096,1024]{1,0:T(8,128)(2,1)}) custom-call(bf16[4096,1024]{1,0:T(8,128)(2,1)} %bitcast.2, bf16[2,1024,2816]{2,1,0:T(8,128)(2,1)} %wg_hbm.3, bf16[2,1024,2816]{2,1,0:T(8,128)(2,1)} %wu_hbm.3, bf16[2,2816,1024]{2,1,0:T(8,128)(2,1)} %wd_hbm.3), custom_call_target="tpu_custom_call" | custom-call | flops 70866960384 | bytes 50855936 | tf_op jit(solution)/shard_map/forward/pallas_call | solution.py:101
  82.1 548.0 %backward.1 = (bf16[2,1024,2816]{2,1,0:T(8,128)(2,1)}, bf16[2,1024,2816]{2,1,0:T(8,128)(2,1)}, bf16[2,2816,1024]{2,1,0:T(8,128)(2,1)}, f32[2,256,2816]{2,1,0:T(8...) custom-call(bf16[4096,1024]{1,0:T(8,128)(2,1)} %get-tuple-element.44, ...), custom_call_target="tpu_custom_call" | custom-call | flops 330712481792 | bytes 184549376 | tf_op jit(solution)/shard_map/backward/pallas_call | solution.py:648
  630.1 1.9 collective-permute-start
  632.0 1.4 collective-permute-start.1
  633.4 0.0 copy-start
  633.4 16.5 %results.3 = (f32[2,256,2816]{2,1,0:T(8,128)}, f32[2,256,2816]{2,1,0:T(8,128)}, f32[2,256,2816]{2,1,0:T(8,128)}, f32[2,256,2816]{2,1,0:T(8,128)}) custom-call(f32[2,256,2816]{2,1,0:T(8,128)} %get-tuple-element.52.refs_0_, f32[2,256,2816]{2,1,0:T(8,128)} %get-tuple-element.53.refs_1_, f32[2,256,2816]{2,1,0:T(8,128)} %get-tuple-element.54.refs_2_, ...), custom_call_target="tpu_custom_call" | custom-call | flops 20000000000 | bytes 46137344 | tf_op jit(solution)/shard_map/results/pallas_call | solution.py:755
  649.9 0.0 copy-done
  649.9 1.7 collective-permute-start.4
  651.7 0.4 collective-permute-start.5
  652.0 16.6 %results.4 = (f32[2,704,1024]{2,1,0:T(8,128)}, f32[2,704,1024]{2,1,0:T(8,128)}, bf16[2,2816,1024]{2,1,0:T(8,128)(2,1)}) custom-call(f32[2,704,1024]{2,1,0:T(8,128)} %get-tuple-element.49.refs_0_, f32[2,704,1024]{2,1,0:T(8,128)} %get-tuple-element.50.refs_1_, bf16[2,2816,1024]{2,1,0:T(8,128)(2,1)} %get-tuple-element.51.refs_2_, ...), custom_call_target="tpu_custom_call" | custom-call | flops 20000000000 | bytes 46137344 | tf_op jit(solution)/shard_map/results/pallas_call | solution.py:755
  668.7 0.0 collective-permute-done.refs_4_
  668.7 0.0 collective-permute-done.1.refs_3_
  668.7 0.7 collective-permute-start.2
  669.4 2.6 collective-permute-start.3
  672.0 16.4 %results.5 = (bf16[2,1024,2816]{2,1,0:T(8,128)(2,1)}, bf16[2,1024,2816]{2,1,0:T(8,128)(2,1)}) custom-call(bf16[2,1024,2816]{2,1,0:T(8,128)(2,1)} %get-tuple-element.63.refs_0_, bf16[2,1024,2816]{2,1,0:T(8,128)(2,1)} %get-tuple-element.64.refs_1_, f32[2,704,1024]{2,1,0:T(8,128)} %get-tuple-element.40.refs_2_), custom_call_target="tpu_custom_call" | custom-call | flops 20000000000 | bytes 46137344 | tf_op jit(solution)/shard_map/results/pallas_call | solution.py:755
  688.4 0.0 collective-permute-done.4.refs_2_
  688.4 0.0 collective-permute-done.5.refs_5_
  688.4 6.1 place_kept.2
  694.6 1.5 collective-permute-done.2.refs_0_
  696.1 0.0 collective-permute-done.3.refs_1_
  696.1 3.0 place_kept.3
Async XLA Ops:
  630.1 38.6 %collective-permute-start = (bf16[2048,256]{1,0:T(8,128)(2,1)}, bf16[2048,256]{1,0:T(8,128)(2,1)}, u32[]{:S(2)}, u32[]{:S(2)}) collective-permute-start(bf16[2048,256]{1,0:T(8,128)(2,1)} %get-tuple-element.61.refs_4_.refs_0_), channel_id=1, source_target_pairs={{0,1},{1,2},{2,3},{3,0},{4,5},{5,6},{6,7},{7,4},{8,9},{9,10},{10,1... | collective-permute-start | bytes 3145736 | tf_op jit(solution)/shard_map/ppermute | solution.py:823
  632.0 36.7 %collective-permute-start.1 = (bf16[2048,256]{1,0:T(8,128)(2,1)}, bf16[2048,256]{1,0:T(8,128)(2,1)}, u32[]{:S(2)}, u32[]{:S(2)}) collective-permute-start(bf16[2048,256]{1,0:T(8,128)(2,1)} %get-tuple-element.62.refs_1_), channel_id=1, source_target_pairs={{0,3},{1,0},{2,1},{3,2},{4,7},{5,4},{6,5},{7,6},{8,11},{9,8},{10,9... | collective-permute-start | bytes 3145736 | tf_op jit(solution)/shard_map/ppermute | solution.py:823
  633.4 16.5 %copy-start = (bf16[2048,256]{1,0:T(8,128)(2,1)S(1)}, bf16[2048,256]{1,0:T(8,128)(2,1)}, u32[]{:S(2)}) copy-start(bf16[2048,256]{1,0:T(8,128)(2,1)} %get-tuple-element.61.refs_4_.refs_0_) | copy-start | bytes 3145732
  649.9 38.5 %collective-permute-start.4 = (bf16[2048,256]{1,0:T(8,128)(2,1)S(1)}, bf16[2048,256]{1,0:T(8,128)(2,1)}, u32[]{:S(2)}, u32[]{:S(2)}) collective-permute-start(bf16[2048,256]{1,0:T(8,128)(2,1)S(1)} %copy-done), channel_id=1, source_target_pairs={{0,3},{1,0},{2,1},{3,2},{4,7},{5,4},{6,5},{7,6},{8,11},{9,8},{10,9... | collective-permute-start | bytes 3145736 | tf_op jit(solution)/shard_map/ppermute | solution.py:826
  651.7 36.7 %collective-permute-start.5 = (bf16[2048,256]{1,0:T(8,128)(2,1)}, bf16[2048,256]{1,0:T(8,128)(2,1)}, u32[]{:S(2)}, u32[]{:S(2)}) collective-permute-start(bf16[2048,256]{1,0:T(8,128)(2,1)} %get-tuple-element.62.refs_1_), channel_id=1, source_target_pairs={{0,1},{1,2},{2,3},{3,0},{4,5},{5,6},{6,7},{7,4},{8,9},{9,10},{10,1... | collective-permute-start | bytes 3145736 | tf_op jit(solution)/shard_map/ppermute | solution.py:826
  668.7 27.4 %collective-permute-start.2 = (bf16[2048,256]{1,0:T(8,128)(2,1)}, bf16[2048,256]{1,0:T(8,128)(2,1)}, u32[]{:S(2)}, u32[]{:S(2)}) collective-permute-start(bf16[2048,256]{1,0:T(8,128)(2,1)} %collective-permute-done.refs_4_), channel_id=1, source_target_pairs={{0,1},{1,2},{2,3},{3,0},{4,5},{5,6},{6,7},{7,4},{8,9},{9,10},{10,1... | collective-permute-start | bytes 3145736 | tf_op jit(solution)/shard_map/ppermute | solution.py:829
  669.4 26.7 %collective-permute-start.3 = (bf16[2048,256]{1,0:T(8,128)(2,1)}, bf16[2048,256]{1,0:T(8,128)(2,1)}, u32[]{:S(2)}, u32[]{:S(2)}) collective-permute-start(bf16[2048,256]{1,0:T(8,128)(2,1)} %collective-permute-done.1.refs_3_), channel_id=1, source_target_pairs={{0,3},{1,0},{2,1},{3,2},{4,7},{5,4},{6,5},{7,6},{8,11},{9,8},{10,9... | collective-permute-start | bytes 3145736 | tf_op jit(solution)/shard_map/ppermute | solution.py:829
